TPU v7x, 32 devices: a whole 2x2x4 slice. The times are simulated.
32 devices in a mesh: layer: 4 (over z), latent: 8 (over y, x, core).
Axes of the slice: x: 2, y: 2, z: 4, core: 2. Of those that a mesh axis runs over, the one named last changes fastest.
Arguments:
- acts: float32 [4, 64, 2304], P('layer', 'latent'), may hold values from -6 to 6
- w_enc: float32 [4, 2304, 2048], P('layer', None, 'latent'), may hold values from -0.0625 to 0.0625
- b_enc: float32 [2048], P('latent'), may hold values from -3 to 3
- w_dec: float32 [2048, 4, 2304], P('latent', 'layer'), may hold values from -0.125 to 0.125
- b_dec: float32 [4, 2304], P('layer'), may hold values from -3 to 3
Outputs:
- grad_enc: float32 [4, 2304, 2048], P('layer', None, 'latent')
- grad_benc: float32 [2048], P('latent')
All inputs are finite; a program needn't handle non-finite values.
Results may differ from a plain program's by a relative error of at most 0.000076.
Values sent between devices are 32-bit elements; how exact they have to be, the bound alone decides.
No kernel may reach another device: no remote copies, remote signals or barrier semaphores. Data moves between devices by JAX's collectives and lax.ppermute only.
A program may use at most 64 MiB of HBM per device.

v0:
```python
import functools

import jax
import jax.numpy as jnp
from jax import lax
from jax.experimental import pallas as pl
from jax.experimental.pallas import tpu as pltpu
from jax.sharding import PartitionSpec as P


SHARP = 4.0
DIRECT_MAX = 8
CHUNK = 256
LANES, PAIR = 128, 16
LIMIT = 30 * 2**20
F32, BF16 = jnp.float32, jnp.bfloat16


def split(x):
    high = x.astype(BF16)
    return high, (x - high.astype(F32)).astype(BF16)


def stacked(x):
    return jnp.concatenate(split(x), axis=0)


def dot(a, b, dims):
    return lax.dot_general(a, b, (dims, ((), ())), preferred_element_type=F32)


def fold(x):
    half = x.shape[0] // 2
    return x[:half] + x[half:]


def call(kernel, outs, args, flops, scratch=()):
    outs = tuple(jax.ShapeDtypeStruct(*o) for o in outs)
    moved = sum(a.size * a.dtype.itemsize for a in args + outs)
    return call_in_vmem(kernel, outs, args, flops, moved, scratch)


def call_in_vmem(kernel, outs, args, flops, moved, scratch):
    return pl.pallas_call(
        kernel,
        out_shape=outs,
        in_specs=[pl.BlockSpec(memory_space=pltpu.VMEM)] * len(args),
        out_specs=[pl.BlockSpec(memory_space=pltpu.VMEM)] * len(outs),
        scratch_shapes=scratch,
        compiler_params=pltpu.CompilerParams(vmem_limit_bytes=LIMIT),
        cost_estimate=pl.CostEstimate(flops=flops, bytes_accessed=moved, transcendentals=0),
    )(*args)


def rows_of(refs):
    return jnp.concatenate([r[...] for r in refs], axis=0) if len(refs) > 1 else refs[0][...]


def encode_kernel(n, *refs):
    blocks, (own_high, own_low, other, out) = refs[:n], refs[n:]
    left = stacked(rows_of(blocks))
    width = other.shape[1]
    totals = [None, None]
    for start in range(0, other.shape[0], CHUNK):
        here = slice(start, start + CHUNK)
        part = left[:, here]
        rights = ((own_high[here, :], own_low[here, :]), split(other[here, :]))
        for at in range(2):
            for right in rights[at]:
                term = dot(part, right, ((1,), (0,)))
                totals[at] = term if totals[at] is None else totals[at] + term
    for at in range(2):
        out[:, at * width : (at + 1) * width] = fold(totals[at])


def prepare_kernel(own, other, high, low, high_turned, low_turned, norms, squares):
    features = high.shape[1]
    runs = features // LANES
    rows = own.shape[0] // runs
    for at, w in enumerate((own, other)):

        def group(g, carry, at=at, w=w):
            total = jnp.zeros((PAIR, LANES), F32)
            here = pl.ds(pl.multiple_of(at * rows + g * PAIR, PAIR), PAIR)
            for j in range(runs):
                x = w[pl.ds(g * (PAIR * runs) + j, PAIR, stride=runs), :]
                lanes = slice(j * LANES, (j + 1) * LANES)
                high[here, lanes], low[here, lanes] = split(x)
                total = total + x * x
            squares[here, :] = total
            return carry

        lax.fori_loop(0, rows // PAIR, group, 0)
    sums = lax.dot_general(
        jnp.ones((8, LANES), F32),
        squares[...],
        (((1,), (1,)), ((), ())),
        precision=lax.Precision.HIGHEST,
        preferred_element_type=F32,
    )
    norms[...] = jnp.sqrt(sums[:1])
    for start in range(0, features, CHUNK):
        here = slice(start, start + CHUNK)
        high_turned[here, :] = high[:, here].T
        low_turned[here, :] = low[:, here].T


def columns_of(refs):
    spans, first = [], 0
    for ref in refs:
        spans.append((ref, first, first + ref.shape[1]))
        first += ref.shape[1]
    return spans


def crossed(x, mask, rows):
    blocks = range(x.shape[0] // rows)
    return jnp.concatenate([x[(b ^ mask) * rows : ((b ^ mask) + 1) * rows] for b in blocks], axis=0)


def decode_kernel(n, *refs):
    parts, (bias, high, low, gate), outs = refs[:n], refs[n : n + 4], refs[n + 4 :]
    pre = parts[0][...]
    for p in parts[1:]:
        pre = pre + p[...]
    scaled = SHARP * (pre + bias[...])
    decay = jnp.exp(-jnp.abs(scaled))
    codes = (jnp.maximum(scaled, 0.0) + jnp.log1p(decay)) / SHARP
    gate[...] = jnp.where(scaled >= 0, 1.0, decay) / (1.0 + decay)
    left = stacked(codes)
    for start in range(0, high.shape[1], CHUNK):
        here = slice(start, start + CHUNK)
        share = fold(
            dot(left, high[:, here], ((1,), (0,))) + dot(left, low[:, here], ((1,), (0,)))
        )
        for out, first, last in columns_of(outs):
            low_end, high_end = max(start, first), min(start + CHUNK, last)
            if low_end < high_end:
                out[:, low_end - first : high_end - first] = share[
                    :, low_end - start : high_end - start
                ]


def gradient_kernel(n, masks, rows, *refs):
    blocks, (shift, high, low, norms), pieces, out = refs[:n], refs[n : n + 4], refs[n + 4 : -1], refs[-1]
    recon = []
    for mask in masks:
        held, *pieces = pieces
        total = held[...]
        if mask:
            other, *pieces = pieces
            total = total + crossed(other[...], mask, rows)
        recon.append(total)
    left = stacked(jnp.concatenate(recon, axis=1) + shift[...] - rows_of(blocks))
    total = None
    for start in range(0, high.shape[0], CHUNK):
        here = slice(start, start + CHUNK)
        for right in (high, low):
            term = dot(left[:, here], right[here, :], ((1,), (0,)))
            total = term if total is None else total + term
    out[...] = fold(total) + norms[...]


def turn_kernel(n, *refs):
    own, (other, out) = refs[:n], refs[n:]
    x = jnp.concatenate([rows_of(own), other[...]], axis=0)
    high, low = split(x)
    out[...] = jnp.concatenate([high, low, high, low], axis=0).T


def weight_kernel(tile, turned, mine, theirs, out, bias, right, result, sem):
    grad = jnp.concatenate([mine[...], theirs[...]], axis=0)
    bias[...] = jnp.sum(grad, axis=0, keepdims=True)
    high, low = split(grad)
    right[...] = jnp.concatenate([high, high, low, low], axis=0)
    copies = []
    for at in range(sem.shape[0]):
        here = slice(at * tile, (at + 1) * tile)
        result[here, :] = dot(turned[here, :], right[...], ((1,), (0,)))
        copies.append(pltpu.make_async_copy(result.at[here, :], out.at[here, :], sem.at[at]))
        copies[-1].start()
    for copy in copies:
        copy.wait()


def weight_gradient(turned, mine, theirs):
    features, depth = turned.shape
    width = mine.shape[1]
    steps = next(n for n in (6, 4, 3, 2, 1) if features % (8 * n) == 0)
    vmem = pl.BlockSpec(memory_space=pltpu.VMEM)
    return pl.pallas_call(
        functools.partial(weight_kernel, features // steps),
        out_shape=(
            jax.ShapeDtypeStruct((features, width), F32),
            jax.ShapeDtypeStruct((1, width), F32),
        ),
        in_specs=[vmem] * 3,
        out_specs=[pl.BlockSpec(memory_space=pltpu.HBM), vmem],
        scratch_shapes=[
            pltpu.VMEM((depth, width), BF16),
            pltpu.VMEM((features, width), F32),
            pltpu.SemaphoreType.DMA((steps,)),
        ],
        compiler_params=pltpu.CompilerParams(vmem_limit_bytes=LIMIT),
        cost_estimate=pl.CostEstimate(
            flops=2 * features * depth * width,
            bytes_accessed=features * (depth * 2 + width * 4),
            transcendentals=0,
        ),
        name="weight_gradient",
    )(turned, mine, theirs)


def on_device(layers, latents, acts, w_enc, b_enc, w_dec, b_dec):
    chips = latents // 2
    direct = chips <= DIRECT_MAX and chips & (chips - 1) == 0
    steps = chips.bit_length() - 1
    same_core = [[2 * j + c for j in range(chips)] for c in range(2)]

    def to_partner(x):
        return lax.ppermute(x, "latent", [(i, i ^ 1) for i in range(latents)])

    def to_chip(x, k):
        return lax.ppermute(x, "latent", [(i, i ^ (2 * k)) for i in range(latents)])

    def gather_chips(x):
        if direct:
            return [x] + [to_chip(x, k) for k in range(1, chips)]
        return [lax.all_gather(x, "latent", axis=0, tiled=True, axis_index_groups=same_core)]

    def sum_chips(shares, rows):
        if not direct or chips == 1:
            if not direct:
                shares = [lax.psum(x, "latent", axis_index_groups=same_core) for x in shares]
            return [0] * len(shares), list(shares)
        held, other = list(shares), [None] * len(shares)
        for step in range(steps):
            for at in range(len(held)):
                mask = 1 << ((step + at) % steps)
                if step:
                    before = 1 << ((step - 1 + at) % steps)
                    held[at] = held[at] + crossed(other[at], before, rows)
                other[at] = to_chip(held[at], mask)
        masks = [1 << ((steps - 1 + at) % steps) for at in range(len(held))]
        return masks, [x for pair in zip(held, other) for x in pair]

    def from_layers(x):
        near = list(range(1, layers))
        if layers == 4:
            orders = ((1, 3, 2), (3, 2, 1))
        else:
            orders = (near, near)
        got = [x]
        for step in range(layers - 1):
            pairs = []
            for layer in range(layers):
                for at in range(latents):
                    k = orders[at & 1][step]
                    to = layer ^ k if layers & (layers - 1) == 0 else (layer + k) % layers
                    pairs.append((layer * latents + at, to * latents + at))
            got.append(lax.ppermute(x, ("layer", "latent"), pairs))
        return got

    enc, local = w_enc[0], acts[0]
    rows, features = local.shape
    width = enc.shape[1]
    tokens = rows * chips
    work = 4 * 2 * tokens * features * 2 * width
    dec = w_dec.reshape(width * features // LANES, LANES)

    other_enc = to_partner(enc)
    other_dec = to_partner(dec)
    received = gather_chips(local)
    rounded = lax.reduce_precision(enc, 8, 7)
    own_high, own_low = rounded.astype(BF16), (enc - rounded).astype(BF16)
    gathered = received
    (partial,) = call(
        functools.partial(encode_kernel, len(gathered)),
        [((tokens, 2 * width), F32)],
        (*gathered, own_high, own_low, other_enc),
        work,
    )
    first = lax.optimization_barrier((b_enc, partial))[0]
    extra = jnp.pad(first[None, :], ((0, 7), (0, features - width)))
    packed = jnp.concatenate(gathered + [extra], axis=0)
    packed = to_partner(packed)
    high, low, high_turned, low_turned, norms = call(
        prepare_kernel,
        [((2 * width, features), BF16)] * 2
        + [((features, 2 * width), BF16)] * 2
        + [((1, 2 * width), F32)],
        (dec, other_dec),
        work,
        (pltpu.VMEM((2 * width, LANES), F32),),
    )
    parts, packed = lax.optimization_barrier((from_layers(partial), packed))
    bias = jnp.concatenate([b_enc, packed[tokens, :width]])[None, :]
    sets = steps if direct and steps > 1 and features % (steps * LANES) == 0 else 1
    gate, *shares = call(
        functools.partial(decode_kernel, len(parts)),
        [((tokens, 2 * width), F32)] + [((tokens, features // sets), F32)] * sets,
        (*parts, bias, high, low),
        work,
    )
    (turned,) = call(
        functools.partial(turn_kernel, len(gathered)),
        [((features, 8 * tokens), BF16)],
        (*gathered, packed[:tokens]),
        work,
    )
    masks, pieces = sum_chips(shares, rows)
    pieces, turned = lax.optimization_barrier((pieces, turned))
    (grad_part,) = call(
        functools.partial(gradient_kernel, len(gathered), masks, rows),
        [((tokens, 2 * width), F32)],
        (*gathered, b_dec, high_turned, low_turned, norms, *pieces),
        work,
    )
    code_grad = sum(from_layers(grad_part)[1:], grad_part)
    pre_grad = code_grad * gate
    theirs = to_partner(pre_grad[:, width:])
    grad, grad_bias = weight_gradient(turned, pre_grad[:, :width], theirs)
    return (grad[None, :, :], grad_bias[0])


def solution(mesh):
    layers, latents = mesh.shape["layer"], mesh.shape["latent"]

    def body(*args):
        return on_device(layers, latents, *args)

    return jax.shard_map(
        body,
        mesh=mesh,
        in_specs=(
            P("layer", "latent", None),
            P("layer", None, "latent"),
            P("latent"),
            P("latent", "layer", None),
            P("layer", None),
        ),
        out_specs=(P("layer", None, "latent"), P("latent")),
        check_vma=False,
    )
```

profile of v0, /device:TPU:0, one launch (start us, length us, event | category | flops | bytes accessed | tf_op | source)
XLA Modules:
  0.0 48.9 jit_solution(15795918750012644650)
XLA Ops:
  0.6 3.0 %collective-permute-start = (f32[8,2304]{1,0:T(8,128)}, f32[8,2304]{1,0:T(8,128)S(1)}, u32[]{:S(2)}, u32[]{:S(2)}) collective-permute-start(f32[8,2304]{1,0:T(8,128)} %bitcast.13), channel_id=1, source_target_pairs={{0,2},{1,3},{2,0},{3,1},{4,6},{5,7},{6,4},{7,5},{8,10},{9,11},{10,... | collective-permute-start | bytes 221192 | tf_op jit(solution)/shard_map/ppermute | solution.py:224
  3.7 1.5 %collective-permute-start.1 = (f32[8,2304]{1,0:T(8,128)}, f32[8,2304]{1,0:T(8,128)S(1)}, u32[]{:S(2)}, u32[]{:S(2)}) collective-permute-start(f32[8,2304]{1,0:T(8,128)} %bitcast.14), channel_id=1, source_target_pairs={{0,4},{1,5},{2,6},{3,7},{4,0},{5,1},{6,2},{7,3},{8,12},{9,13},{10,... | collective-permute-start | bytes 221192 | tf_op jit(solution)/shard_map/ppermute | solution.py:224
  5.2 0.5 %collective-permute-start.8 = (f32[4608,128]{1,0:T(8,128)}, f32[4608,128]{1,0:T(8,128)S(1)}, u32[]{:S(2)}, u32[]{:S(2)}) collective-permute-start(f32[4608,128]{1,0:T(8,128)} %bitcast.11), channel_id=1, source_target_pairs={{0,1},{1,0},{2,3},{3,2},{4,5},{5,4},{6,7},{7,6},{8,9},{9,8},{10,11... | collective-permute-start | bytes 7077896 | tf_op jit(solution)/shard_map/ppermute | solution.py:221
  5.7 2.0 %fusion = (bf16[2304,256]{1,0:T(8,128)(2,1)S(1)}, bf16[2304,256]{1,0:T(8,128)(2,1)S(1)}) fusion(f32[1,2304,256]{2,1,0:T(8,128)} %param.6), kind=kLoop, calls=%fused_computation.2 | loop fusion | flops 2359296 | bytes 4718592 | tf_op jit(solution)/shard_map/convert_element_type | solution.py:275
  7.8 0.4 collective-permute-done.1.refs_2_
  8.2 2.4 %collective-permute-done.2.refs_3_ = f32[8,2304]{1,0:T(8,128)S(1)} collective-permute-done((f32[8,2304]{1,0:T(8,128)}, f32[8,2304]{1,0:T(8,128)S(1)}, u32[]{:S(2)}, u32[]{:S(2)}) %collective-permute-start.2) | collective-permute-done | bytes 73760 | tf_op jit(solution)/shard_map/ppermute | solution.py:224
  10.7 0.9 %shard_map.68.refs_0_ = f32[32,512]{1,0:T(8,128)S(1)} custom-call(f32[8,2304]{1,0:T(8,128)S(1)} %bitcast.16, f32[8,2304]{1,0:T(8,128)S(1)} %collective-permute-done.refs_1_, f32[8,2304]{1,0:T(8,128)S(1)} %collective-permute-done.1.refs_2_, f32[8,2304]{1,0:T(8,128)S(1)} %collective-permute-done.2.refs_3_, bf16[2304,256]{1,0:T(8,128)(2,1)S(1)} %get-tuple-element.45.refs_4_, ...), custom_call_target="tpu_custom_call" | custom-call | flops 301989888 | bytes 5079040 | tf_op jit(solution)/shard_map/pallas_call | solution.py:44
  11.7 1.6 %collective-permute-start.4 = (f32[32,512]{1,0:T(8,128)S(1)}, f32[32,512]{1,0:T(8,128)S(1)}, u32[]{:S(2)}, u32[]{:S(2)}) collective-permute-start(f32[32,512]{1,0:T(8,128)S(1)} %shard_map.68.refs_0_), channel_id=1, source_target_pairs={{0,8},{1,25},{2,10},{3,27},{4,12},{5,29},{6,14},{7,31},{8,0},{9,17... | collective-permute-start | bytes 196616 | tf_op jit(solution)/shard_map/ppermute | solution.py:261
  13.4 2.5 %collective-permute-start.5 = (f32[32,512]{1,0:T(8,128)S(1)}, f32[32,512]{1,0:T(8,128)S(1)}, u32[]{:S(2)}, u32[]{:S(2)}) collective-permute-start(f32[32,512]{1,0:T(8,128)S(1)} %shard_map.68.refs_0_), channel_id=1, source_target_pairs={{0,24},{1,17},{2,26},{3,19},{4,28},{5,21},{6,30},{7,23},{8,16},{9,... | collective-permute-start | bytes 196616 | tf_op jit(solution)/shard_map/ppermute | solution.py:261
  15.8 0.1 collective-permute-start.6
  16.0 2.5 %shard_map.69 = (bf16[512,2304]{1,0:T(8,128)(2,1)S(1)}, bf16[512,2304]{1,0:T(8,128)(2,1)S(1)}, bf16[2304,512]{1,0:T(8,128)(2,1)S(1)}, bf16[2304,512]{1,0:T(8,128)(2,1)S(1)}, f32[1,512]{1,0:T(1,128)S(1)}) custom-call(f32[4608,128]{1,0:T(8,128)S(1)} %bitcast.12, f32[4608,128]{1,0:T(8,128)S(1)} %collective-permute-done.8.other), custom_call_target="tpu_custom_call" | custom-call | flops 301989888 | bytes 14157824 | tf_op jit(solution)/shard_map/pallas_call | solution.py:44
  18.5 1.1 %collective-permute-done.5.refs_2_ = f32[32,512]{1,0:T(8,128)S(1)} collective-permute-done((f32[32,512]{1,0:T(8,128)S(1)}, f32[32,512]{1,0:T(8,128)S(1)}, u32[]{:S(2)}, u32[]{:S(2)}) %collective-permute-start.5) | collective-permute-done | bytes 65568 | tf_op jit(solution)/shard_map/ppermute | solution.py:261
  19.6 1.9 %collective-permute-done.6.refs_3_ = f32[32,512]{1,0:T(8,128)S(1)} collective-permute-done((f32[32,512]{1,0:T(8,128)S(1)}, f32[32,512]{1,0:T(8,128)S(1)}, u32[]{:S(2)}, u32[]{:S(2)}) %collective-permute-start.6) | collective-permute-done | bytes 65568 | tf_op jit(solution)/shard_map/ppermute | solution.py:261
  21.5 0.9 %shard_map.70 = (f32[32,512]{1,0:T(8,128)S(1)}, f32[32,1152]{1,0:T(8,128)S(1)}, f32[32,1152]{1,0:T(8,128)S(1)}) custom-call(f32[32,512]{1,0:T(8,128)S(1)} %shard_map.68.refs_0_, f32[32,512]{1,0:T(8,128)S(1)} %collective-permute-done.4.refs_1_, f32[32,512]{1,0:T(8,128)S(1)} %collective-permute-done.5.refs_2_, f32[32,512]{1,0:T(8,128)S(1)} %collective-permute-done.6.refs_3_, ...), custom_call_target="tpu_custom_call" | custom-call | flops 301989888 | bytes 5343232 | tf_op jit(solution)/shard_map/pallas_call | solution.py:44
  22.4 1.5 %collective-permute-start.11 = (f32[32,1152]{1,0:T(8,128)S(1)}, f32[32,1152]{1,0:T(8,128)S(1)}, u32[]{:S(2)}, u32[]{:S(2)}) collective-permute-start(f32[32,1152]{1,0:T(8,128)S(1)} %get-tuple-element.32), channel_id=1, source_target_pairs={{0,4},{1,5},{2,6},{3,7},{4,0},{5,1},{6,2},{7,3},{8,12},{9,13},{10,... | collective-permute-start | bytes 442376 | tf_op jit(solution)/shard_map/ppermute | solution.py:224
  24.0 1.5 %collective-permute-start.9 = (f32[32,1152]{1,0:T(8,128)S(1)}, f32[32,1152]{1,0:T(8,128)S(1)}, u32[]{:S(2)}, u32[]{:S(2)}) collective-permute-start(f32[32,1152]{1,0:T(8,128)S(1)} %get-tuple-element.31), channel_id=1, source_target_pairs={{0,2},{1,3},{2,0},{3,1},{4,6},{5,7},{6,4},{7,5},{8,10},{9,11},{10,... | collective-permute-start | bytes 442376 | tf_op jit(solution)/shard_map/ppermute | solution.py:224
  25.5 2.2 %collective-permute-done.11 = f32[32,1152]{1,0:T(8,128)S(1)} collective-permute-done((f32[32,1152]{1,0:T(8,128)S(1)}, f32[32,1152]{1,0:T(8,128)S(1)}, u32[]{:S(2)}, u32[]{:S(2)}) %collective-permute-start.11) | collective-permute-done | bytes 147488 | tf_op jit(solution)/shard_map/ppermute | solution.py:224
  27.6 1.5 %collective-permute-start.12 = (f32[32,1152]{1,0:T(8,128)S(1)}, f32[32,1152]{1,0:T(8,128)S(1)}, u32[]{:S(2)}, u32[]{:S(2)}) collective-permute-start(f32[32,1152]{1,0:T(8,128)S(1)} %maximum_add_fusion.1.refs_10_), channel_id=1, source_target_pairs={{0,2},{1,3},{2,0},{3,1},{4,6},{5,7},{6,4},{7,5},{8,10},{9,11},{10,... | collective-permute-start | bytes 442376 | tf_op jit(solution)/shard_map/ppermute | solution.py:224
  29.2 1.2 %collective-permute-done.9 = f32[32,1152]{1,0:T(8,128)S(1)} collective-permute-done((f32[32,1152]{1,0:T(8,128)S(1)}, f32[32,1152]{1,0:T(8,128)S(1)}, u32[]{:S(2)}, u32[]{:S(2)}) %collective-permute-start.9) | collective-permute-done | bytes 147488 | tf_op jit(solution)/shard_map/ppermute | solution.py:224
  30.5 0.3 collective-permute-start.10
  30.8 0.2 shard_map.71.turned
  31.0 1.8 %collective-permute-done.12.refs_11_ = f32[32,1152]{1,0:T(8,128)S(1)} collective-permute-done((f32[32,1152]{1,0:T(8,128)S(1)}, f32[32,1152]{1,0:T(8,128)S(1)}, u32[]{:S(2)}, u32[]{:S(2)}) %collective-permute-start.12) | collective-permute-done | bytes 147488 | tf_op jit(solution)/shard_map/ppermute | solution.py:224
  32.9 2.8 %collective-permute-done.10.refs_9_ = f32[32,1152]{1,0:T(8,128)S(1)} collective-permute-done((f32[32,1152]{1,0:T(8,128)S(1)}, f32[32,1152]{1,0:T(8,128)S(1)}, u32[]{:S(2)}, u32[]{:S(2)}) %collective-permute-start.10) | collective-permute-done | bytes 147488 | tf_op jit(solution)/shard_map/ppermute | solution.py:224
  35.7 0.9 %shard_map.72 = f32[32,512]{1,0:T(8,128)S(1)} custom-call(f32[8,2304]{1,0:T(8,128)S(1)} %bitcast.18, f32[8,2304]{1,0:T(8,128)S(1)} %collective-permute-done.refs_1_, f32[8,2304]{1,0:T(8,128)S(1)} %collective-permute-done.1.refs_2_, f32[8,2304]{1,0:T(8,128)S(1)} %collective-permute-done.2.refs_3_, f32[1,2304]{1,0:T(1,128)S(1)} %copy-done.2, ...), custom_call_target="tpu_custom_call" | custom-call | flops 301989888 | bytes 5680128 | tf_op jit(solution)/shard_map/pallas_call | solution.py:44
  36.6 2.9 %collective-permute-start.14 = (f32[32,512]{1,0:T(8,128)S(1)}, f32[32,512]{1,0:T(8,128)S(1)}, u32[]{:S(2)}, u32[]{:S(2)}) collective-permute-start(f32[32,512]{1,0:T(8,128)S(1)} %shard_map.72), channel_id=1, source_target_pairs={{0,24},{1,17},{2,26},{3,19},{4,28},{5,21},{6,30},{7,23},{8,16},{9,... | collective-permute-start | bytes 196616 | tf_op jit(solution)/shard_map/ppermute | solution.py:261
  39.5 0.6 %collective-permute-start.15 = (f32[32,512]{1,0:T(8,128)S(1)}, f32[32,512]{1,0:T(8,128)S(1)}, u32[]{:S(2)}, u32[]{:S(2)}) collective-permute-start(f32[32,512]{1,0:T(8,128)S(1)} %shard_map.72), channel_id=1, source_target_pairs={{0,16},{1,9},{2,18},{3,11},{4,20},{5,13},{6,22},{7,15},{8,24},{9,1... | collective-permute-start | bytes 196616 | tf_op jit(solution)/shard_map/ppermute | solution.py:261
  40.1 0.8 %collective-permute-done.13 = f32[32,512]{1,0:T(8,128)S(1)} collective-permute-done((f32[32,512]{1,0:T(8,128)S(1)}, f32[32,512]{1,0:T(8,128)S(1)}, u32[]{:S(2)}, u32[]{:S(2)}) %collective-permute-start.13) | collective-permute-done | bytes 65568 | tf_op jit(solution)/shard_map/ppermute | solution.py:261
  40.9 2.0 %collective-permute-done.14 = f32[32,512]{1,0:T(8,128)S(1)} collective-permute-done((f32[32,512]{1,0:T(8,128)S(1)}, f32[32,512]{1,0:T(8,128)S(1)}, u32[]{:S(2)}, u32[]{:S(2)}) %collective-permute-start.14) | collective-permute-done | bytes 65568 | tf_op jit(solution)/shard_map/ppermute | solution.py:261
  42.8 2.5 %collective-permute-done.15 = f32[32,512]{1,0:T(8,128)S(1)} collective-permute-done((f32[32,512]{1,0:T(8,128)S(1)}, f32[32,512]{1,0:T(8,128)S(1)}, u32[]{:S(2)}, u32[]{:S(2)}) %collective-permute-start.15) | collective-permute-done | bytes 65568 | tf_op jit(solution)/shard_map/ppermute | solution.py:261
  45.4 0.1 collective-permute-start.16
  45.5 1.2 %collective-permute-done.16.theirs = f32[32,256]{1,0:T(8,128)S(1)} collective-permute-done((f32[32,256]{1,0:T(8,128)S(1)}, f32[32,256]{1,0:T(8,128)S(1)}, u32[]{:S(2)}, u32[]{:S(2)}) %collective-permute-start.16) | collective-permute-done | bytes 32800 | tf_op jit(solution)/shard_map/ppermute | solution.py:221
  46.7 2.3 %weight_gradient.1 = (f32[2304,256]{1,0:T(8,128)}, f32[1,256]{1,0:T(1,128)}) custom-call(bf16[2304,256]{1,0:T(8,128)(2,1)S(1)} %shard_map.71.turned, f32[32,256]{1,0:T(8,128)S(1)} %get-tuple-element.53.mine, f32[32,256]{1,0:T(8,128)S(1)} %collective-permute-done.16.theirs), custom_call_target="tpu_custom_call" | custom-call | flops 301989888 | bytes 3538944 | tf_op jit(solution)/shard_map/weight_gradient/pallas_call | solution.py:191
  (31 shorter events, 0.3 us)
Async XLA Ops:
  0.6 7.1 %collective-permute-start = (f32[8,2304]{1,0:T(8,128)}, f32[8,2304]{1,0:T(8,128)S(1)}, u32[]{:S(2)}, u32[]{:S(2)}) collective-permute-start(f32[8,2304]{1,0:T(8,128)} %bitcast.13), channel_id=1, source_target_pairs={{0,2},{1,3},{2,0},{3,1},{4,6},{5,7},{6,4},{7,5},{8,10},{9,11},{10,... | collective-permute-start | bytes 221192 | tf_op jit(solution)/shard_map/ppermute | solution.py:224
  3.7 4.6 %collective-permute-start.1 = (f32[8,2304]{1,0:T(8,128)}, f32[8,2304]{1,0:T(8,128)S(1)}, u32[]{:S(2)}, u32[]{:S(2)}) collective-permute-start(f32[8,2304]{1,0:T(8,128)} %bitcast.14), channel_id=1, source_target_pairs={{0,4},{1,5},{2,6},{3,7},{4,0},{5,1},{6,2},{7,3},{8,12},{9,13},{10,... | collective-permute-start | bytes 221192 | tf_op jit(solution)/shard_map/ppermute | solution.py:224
  5.2 5.5 %collective-permute-start.2 = (f32[8,2304]{1,0:T(8,128)}, f32[8,2304]{1,0:T(8,128)S(1)}, u32[]{:S(2)}, u32[]{:S(2)}) collective-permute-start(f32[8,2304]{1,0:T(8,128)} %bitcast.15), channel_id=1, source_target_pairs={{0,6},{1,7},{2,4},{3,5},{4,2},{5,3},{6,0},{7,1},{8,14},{9,15},{10,... | collective-permute-start | bytes 221192 | tf_op jit(solution)/shard_map/ppermute | solution.py:224
  5.2 5.5 %collective-permute-start.3 = (f32[2304,256]{1,0:T(8,128)}, f32[2304,256]{1,0:T(8,128)S(1)}, u32[]{:S(2)}, u32[]{:S(2)}) collective-permute-start(f32[2304,256]{1,0:T(8,128)} %bitcast.20), channel_id=1, source_target_pairs={{0,1},{1,0},{2,3},{3,2},{4,5},{5,4},{6,7},{7,6},{8,9},{9,8},{10,11... | collective-permute-start | bytes 7077896 | tf_op jit(solution)/shard_map/ppermute | solution.py:221
  5.2 2.5 %copy-start.1 = (f32[1,8,2304]{2,1,0:T(8,128)S(1)}, f32[1,8,2304]{2,1,0:T(8,128)}, u32[]{:S(2)}) copy-start(f32[1,8,2304]{2,1,0:T(8,128)} %param.5) | copy-start | bytes 221188
  5.2 10.7 %collective-permute-start.8 = (f32[4608,128]{1,0:T(8,128)}, f32[4608,128]{1,0:T(8,128)S(1)}, u32[]{:S(2)}, u32[]{:S(2)}) collective-permute-start(f32[4608,128]{1,0:T(8,128)} %bitcast.11), channel_id=1, source_target_pairs={{0,1},{1,0},{2,3},{3,2},{4,5},{5,4},{6,7},{7,6},{8,9},{9,8},{10,11... | collective-permute-start | bytes 7077896 | tf_op jit(solution)/shard_map/ppermute | solution.py:221
  10.7 1.0 %copy-start.3 = (f32[256]{0:T(256)S(1)}, f32[256]{0:T(256)}, u32[]{:S(2)}) copy-start(f32[256]{0:T(256)} %param.7) | copy-start | bytes 3076
  10.7 5.3 %copy-start = (f32[256,1,2304]{2,1,0:T(1,128)S(1)}, f32[256,1,2304]{2,1,0:T(1,128)}, u32[]{:S(2)}) copy-start(f32[256,1,2304]{2,1,0:T(1,128)} %param.8) | copy-start | bytes 7077892
  11.6 9.9 %collective-permute-start.7 = (f32[40,2304]{1,0:T(8,128)S(1)}, f32[40,2304]{1,0:T(8,128)S(1)}, u32[]{:S(2)}, u32[]{:S(2)}) collective-permute-start(f32[40,2304]{1,0:T(8,128)S(1)} %pad_dynamic-update-slice_fusion), channel_id=1, source_target_pairs={{0,1},{1,0},{2,3},{3,2},{4,5},{5,4},{6,7},{7,6},{8,9},{9,8},{10,11... | collective-permute-start | bytes 1105928 | tf_op jit(solution)/shard_map/ppermute | solution.py:221
  11.7 6.7 %collective-permute-start.4 = (f32[32,512]{1,0:T(8,128)S(1)}, f32[32,512]{1,0:T(8,128)S(1)}, u32[]{:S(2)}, u32[]{:S(2)}) collective-permute-start(f32[32,512]{1,0:T(8,128)S(1)} %shard_map.68.refs_0_), channel_id=1, source_target_pairs={{0,8},{1,25},{2,10},{3,27},{4,12},{5,29},{6,14},{7,31},{8,0},{9,17... | collective-permute-start | bytes 196616 | tf_op jit(solution)/shard_map/ppermute | solution.py:261
  13.4 6.2 %collective-permute-start.5 = (f32[32,512]{1,0:T(8,128)S(1)}, f32[32,512]{1,0:T(8,128)S(1)}, u32[]{:S(2)}, u32[]{:S(2)}) collective-permute-start(f32[32,512]{1,0:T(8,128)S(1)} %shard_map.68.refs_0_), channel_id=1, source_target_pairs={{0,24},{1,17},{2,26},{3,19},{4,28},{5,21},{6,30},{7,23},{8,16},{9,... | collective-permute-start | bytes 196616 | tf_op jit(solution)/shard_map/ppermute | solution.py:261
  15.8 5.7 %collective-permute-start.6 = (f32[32,512]{1,0:T(8,128)S(1)}, f32[32,512]{1,0:T(8,128)S(1)}, u32[]{:S(2)}, u32[]{:S(2)}) collective-permute-start(f32[32,512]{1,0:T(8,128)S(1)} %shard_map.68.refs_0_), channel_id=1, source_target_pairs={{0,16},{1,9},{2,18},{3,11},{4,20},{5,13},{6,22},{7,15},{8,24},{9,1... | collective-permute-start | bytes 196616 | tf_op jit(solution)/shard_map/ppermute | solution.py:261
  22.4 13.2 %copy-start.2 = (f32[1,2304]{1,0:T(1,128)S(1)}, f32[1,2304]{1,0:T(1,128)}, u32[]{:S(2)}) copy-start(f32[1,2304]{1,0:T(1,128)} %refs_4_.1) | copy-start | bytes 27652
  22.4 5.2 %collective-permute-start.11 = (f32[32,1152]{1,0:T(8,128)S(1)}, f32[32,1152]{1,0:T(8,128)S(1)}, u32[]{:S(2)}, u32[]{:S(2)}) collective-permute-start(f32[32,1152]{1,0:T(8,128)S(1)} %get-tuple-element.32), channel_id=1, source_target_pairs={{0,4},{1,5},{2,6},{3,7},{4,0},{5,1},{6,2},{7,3},{8,12},{9,13},{10,... | collective-permute-start | bytes 442376 | tf_op jit(solution)/shard_map/ppermute | solution.py:224
  24.0 6.5 %collective-permute-start.9 = (f32[32,1152]{1,0:T(8,128)S(1)}, f32[32,1152]{1,0:T(8,128)S(1)}, u32[]{:S(2)}, u32[]{:S(2)}) collective-permute-start(f32[32,1152]{1,0:T(8,128)S(1)} %get-tuple-element.31), channel_id=1, source_target_pairs={{0,2},{1,3},{2,0},{3,1},{4,6},{5,7},{6,4},{7,5},{8,10},{9,11},{10,... | collective-permute-start | bytes 442376 | tf_op jit(solution)/shard_map/ppermute | solution.py:224
  27.6 5.2 %collective-permute-start.12 = (f32[32,1152]{1,0:T(8,128)S(1)}, f32[32,1152]{1,0:T(8,128)S(1)}, u32[]{:S(2)}, u32[]{:S(2)}) collective-permute-start(f32[32,1152]{1,0:T(8,128)S(1)} %maximum_add_fusion.1.refs_10_), channel_id=1, source_target_pairs={{0,2},{1,3},{2,0},{3,1},{4,6},{5,7},{6,4},{7,5},{8,10},{9,11},{10,... | collective-permute-start | bytes 442376 | tf_op jit(solution)/shard_map/ppermute | solution.py:224
  30.5 5.2 %collective-permute-start.10 = (f32[32,1152]{1,0:T(8,128)S(1)}, f32[32,1152]{1,0:T(8,128)S(1)}, u32[]{:S(2)}, u32[]{:S(2)}) collective-permute-start(f32[32,1152]{1,0:T(8,128)S(1)} %maximum_add_fusion.refs_8_), channel_id=1, source_target_pairs={{0,4},{1,5},{2,6},{3,7},{4,0},{5,1},{6,2},{7,3},{8,12},{9,13},{10,... | collective-permute-start | bytes 442376 | tf_op jit(solution)/shard_map/ppermute | solution.py:224
  36.6 4.3 %collective-permute-start.13 = (f32[32,512]{1,0:T(8,128)S(1)}, f32[32,512]{1,0:T(8,128)S(1)}, u32[]{:S(2)}, u32[]{:S(2)}) collective-permute-start(f32[32,512]{1,0:T(8,128)S(1)} %shard_map.72), channel_id=1, source_target_pairs={{0,8},{1,25},{2,10},{3,27},{4,12},{5,29},{6,14},{7,31},{8,0},{9,17... | collective-permute-start | bytes 196616 | tf_op jit(solution)/shard_map/ppermute | solution.py:261
  36.6 6.2 %collective-permute-start.14 = (f32[32,512]{1,0:T(8,128)S(1)}, f32[32,512]{1,0:T(8,128)S(1)}, u32[]{:S(2)}, u32[]{:S(2)}) collective-permute-start(f32[32,512]{1,0:T(8,128)S(1)} %shard_map.72), channel_id=1, source_target_pairs={{0,24},{1,17},{2,26},{3,19},{4,28},{5,21},{6,30},{7,23},{8,16},{9,... | collective-permute-start | bytes 196616 | tf_op jit(solution)/shard_map/ppermute | solution.py:261
  39.5 5.9 %collective-permute-start.15 = (f32[32,512]{1,0:T(8,128)S(1)}, f32[32,512]{1,0:T(8,128)S(1)}, u32[]{:S(2)}, u32[]{:S(2)}) collective-permute-start(f32[32,512]{1,0:T(8,128)S(1)} %shard_map.72), channel_id=1, source_target_pairs={{0,16},{1,9},{2,18},{3,11},{4,20},{5,13},{6,22},{7,15},{8,24},{9,1... | collective-permute-start | bytes 196616 | tf_op jit(solution)/shard_map/ppermute | solution.py:261
  45.4 1.3 %collective-permute-start.16 = (f32[32,256]{1,0:T(8,128)S(1)}, f32[32,256]{1,0:T(8,128)S(1)}, u32[]{:S(2)}, u32[]{:S(2)}) collective-permute-start(f32[32,256]{1,0:T(8,128)S(1)} %get-tuple-element.52), channel_id=1, source_target_pairs={{0,1},{1,0},{2,3},{3,2},{4,5},{5,4},{6,7},{7,6},{8,9},{9,8},{10,11... | collective-permute-start | bytes 98312 | tf_op jit(solution)/shard_map/ppermute | solution.py:221
where the time goes:
time: 49.1 us; the launch traced here: 48.9 us
  waiting for transfers between devices  20.4 us (42%)
  starting transfers between devices  17.8 us (36%)
  Pallas kernels  7.71 us (16%)
  other arithmetic  2.09 us (4%)
  between operations  0.8 us (2%)
    ppermute x7, waiting for transfers between devices, to_chip(): return lax.ppermute(x, 'latent', [(i, i ^ 2 * k) for i in range(latents)])  10.9 us
    ppermute x7, starting transfers between devices, to_chip(): return lax.ppermute(x, 'latent', [(i, i ^ 2 * k) for i in range(latents)])  9.46 us
    ppermute x6, waiting for transfers between devices, from_layers(): got.append(lax.ppermute(x, ('layer', 'latent'), pairs))  8.28 us
    ppermute x6, starting transfers between devices, from_layers(): got.append(lax.ppermute(x, ('layer', 'latent'), pairs))  7.74 us
    pallas_call x5, Pallas kernels, call_in_vmem(): pl.pallas_call(kernel, out_shape=outs, in_specs=[pl.BlockSpec(memory_spac...  5.44 us
    pallas_call x1, Pallas kernels, weight_gradient(): pl.pallas_call(functools.partial(weight_kernel, features // steps), out_s...  2.27 us
    convert_element_type x1, other arithmetic, on_device(): own_high, own_low = (rounded.astype(BF16), (enc - rounded).astype(BF16))  2.02 us
    ppermute x4, waiting for transfers between devices, to_partner(): return lax.ppermute(x, 'latent', [(i, i ^ 1) for i in range(latents)])  1.2 us
  transfers between devices with their start and end apart: 17, of which 12 were waited for; matrix products, arithmetic and copies ran while one was open for 4% of the time, Pallas kernels for 7%

commit v1 on v0

--- a/solution.py
+++ b/solution.py
@@ -245,20 +245,12 @@
         return masks, [x for pair in zip(held, other) for x in pair]
 
     def from_layers(x):
-        near = list(range(1, layers))
-        if layers == 4:
-            orders = ((1, 3, 2), (3, 2, 1))
-        else:
-            orders = (near, near)
         got = [x]
         for step in range(layers - 1):
-            pairs = []
-            for layer in range(layers):
-                for at in range(latents):
-                    k = orders[at & 1][step]
-                    to = layer ^ k if layers & (layers - 1) == 0 else (layer + k) % layers
-                    pairs.append((layer * latents + at, to * latents + at))
-            got.append(lax.ppermute(x, ("layer", "latent"), pairs))
+            k = layers - 1 if step == 0 else step
+            even = layers & (layers - 1) == 0
+            pairs = [(i, i ^ k if even else (i + k) % layers) for i in range(layers)]
+            got.append(lax.ppermute(x, "layer", pairs))
         return got
 
     enc, local = w_enc[0], acts[0]

time: 49.1 us -> 47 us (0.957)
  waiting for transfers between devices: 20.4 us -> 17.3 us
  starting transfers between devices: 17.8 us -> 18.9 us
    ppermute x6, waiting for transfers between devices: 8.28 us -> 5.57 us  [from_layers(): got.append(lax.ppermute(x, 'layer', pairs))]
    ppermute x6, starting transfers between devices: 7.74 us -> 8.86 us  [from_layers(): got.append(lax.ppermute(x, 'layer', pairs))]
  transfers between devices with their start and end apart: 17 -> 17, of which waited for: 12 -> 11; matrix products, arithmetic and copies ran while one was open for 4% -> 5% of each run, Pallas kernels for 7% -> 8%
where the time goes in v1:
time: 47 us; the launch traced here: 46.9 us
  starting transfers between devices  18.9 us (40%)
  waiting for transfers between devices  17.3 us (37%)
  Pallas kernels  7.71 us (16%)
  other arithmetic  2.09 us (4%)
  between operations  0.79 us (2%)
    ppermute x7, waiting for transfers between devices, to_chip(): return lax.ppermute(x, 'latent', [(i, i ^ 2 * k) for i in range(latents)])  10.5 us
    ppermute x7, starting transfers between devices, to_chip(): return lax.ppermute(x, 'latent', [(i, i ^ 2 * k) for i in range(latents)])  9.36 us
    ppermute x6, starting transfers between devices, from_layers(): got.append(lax.ppermute(x, 'layer', pairs))  8.86 us
    ppermute x6, waiting for transfers between devices, from_layers(): got.append(lax.ppermute(x, 'layer', pairs))  5.57 us
    pallas_call x5, Pallas kernels, call_in_vmem(): pl.pallas_call(kernel, out_shape=outs, in_specs=[pl.BlockSpec(memory_spac...  5.44 us
    pallas_call x1, Pallas kernels, weight_gradient(): pl.pallas_call(functools.partial(weight_kernel, features // steps), out_s...  2.27 us
    convert_element_type x1, other arithmetic, on_device(): own_high, own_low = (rounded.astype(BF16), (enc - rounded).astype(BF16))  2.02 us
    ppermute x4, waiting for transfers between devices, to_partner(): return lax.ppermute(x, 'latent', [(i, i ^ 1) for i in range(latents)])  1.2 us
  transfers between devices with their start and end apart: 17, of which 11 were waited for; matrix products, arithmetic and copies ran while one was open for 5% of the time, Pallas kernels for 8%

profile of v1, /device:TPU:0, one launch (start us, length us, event | category | flops | bytes accessed | tf_op | source)
XLA Modules:
  0.0 46.9 jit_solution(17797915168634524550)
XLA Ops:
  0.6 3.0 %collective-permute-start = (f32[8,2304]{1,0:T(8,128)}, f32[8,2304]{1,0:T(8,128)S(1)}, u32[]{:S(2)}, u32[]{:S(2)}) collective-permute-start(f32[8,2304]{1,0:T(8,128)} %bitcast.13), channel_id=1, source_target_pairs={{0,2},{1,3},{2,0},{3,1},{4,6},{5,7},{6,4},{7,5},{8,10},{9,11},{10,... | collective-permute-start | bytes 221192 | tf_op jit(solution)/shard_map/ppermute | solution.py:224
  3.7 1.5 %collective-permute-start.1 = (f32[8,2304]{1,0:T(8,128)}, f32[8,2304]{1,0:T(8,128)S(1)}, u32[]{:S(2)}, u32[]{:S(2)}) collective-permute-start(f32[8,2304]{1,0:T(8,128)} %bitcast.14), channel_id=1, source_target_pairs={{0,4},{1,5},{2,6},{3,7},{4,0},{5,1},{6,2},{7,3},{8,12},{9,13},{10,... | collective-permute-start | bytes 221192 | tf_op jit(solution)/shard_map/ppermute | solution.py:224
  5.2 0.5 %collective-permute-start.8 = (f32[4608,128]{1,0:T(8,128)}, f32[4608,128]{1,0:T(8,128)S(1)}, u32[]{:S(2)}, u32[]{:S(2)}) collective-permute-start(f32[4608,128]{1,0:T(8,128)} %bitcast.11), channel_id=1, source_target_pairs={{0,1},{1,0},{2,3},{3,2},{4,5},{5,4},{6,7},{7,6},{8,9},{9,8},{10,11... | collective-permute-start | bytes 7077896 | tf_op jit(solution)/shard_map/ppermute | solution.py:221
  5.7 2.0 %fusion = (bf16[2304,256]{1,0:T(8,128)(2,1)S(1)}, bf16[2304,256]{1,0:T(8,128)(2,1)S(1)}) fusion(f32[1,2304,256]{2,1,0:T(8,128)} %param.6), kind=kLoop, calls=%fused_computation.2 | loop fusion | flops 2359296 | bytes 4718592 | tf_op jit(solution)/shard_map/convert_element_type | solution.py:267
  7.8 0.4 collective-permute-done.1.refs_2_
  8.2 2.4 %collective-permute-done.2.refs_3_ = f32[8,2304]{1,0:T(8,128)S(1)} collective-permute-done((f32[8,2304]{1,0:T(8,128)}, f32[8,2304]{1,0:T(8,128)S(1)}, u32[]{:S(2)}, u32[]{:S(2)}) %collective-permute-start.2) | collective-permute-done | bytes 73760 | tf_op jit(solution)/shard_map/ppermute | solution.py:224
  10.7 0.9 %shard_map.68.refs_0_ = f32[32,512]{1,0:T(8,128)S(1)} custom-call(f32[8,2304]{1,0:T(8,128)S(1)} %bitcast.16, f32[8,2304]{1,0:T(8,128)S(1)} %collective-permute-done.refs_1_, f32[8,2304]{1,0:T(8,128)S(1)} %collective-permute-done.1.refs_2_, f32[8,2304]{1,0:T(8,128)S(1)} %collective-permute-done.2.refs_3_, bf16[2304,256]{1,0:T(8,128)(2,1)S(1)} %get-tuple-element.45.refs_4_, ...), custom_call_target="tpu_custom_call" | custom-call | flops 301989888 | bytes 5079040 | tf_op jit(solution)/shard_map/pallas_call | solution.py:44
  11.6 0.1 collective-permute-start.7
  11.7 3.7 %collective-permute-start.4 = (f32[32,512]{1,0:T(8,128)S(1)}, f32[32,512]{1,0:T(8,128)S(1)}, u32[]{:S(2)}, u32[]{:S(2)}) collective-permute-start(f32[32,512]{1,0:T(8,128)S(1)} %shard_map.68.refs_0_), channel_id=1, source_target_pairs={{0,24},{8,16},{16,8},{24,0},{1,25},{9,17},{17,9},{25,1},{2,26},{10... | collective-permute-start | bytes 196616 | tf_op jit(solution)/shard_map/ppermute | solution.py:253
  15.4 0.8 %collective-permute-start.6 = (f32[32,512]{1,0:T(8,128)S(1)}, f32[32,512]{1,0:T(8,128)S(1)}, u32[]{:S(2)}, u32[]{:S(2)}) collective-permute-start(f32[32,512]{1,0:T(8,128)S(1)} %shard_map.68.refs_0_), channel_id=1, source_target_pairs={{0,16},{8,24},{16,0},{24,8},{1,17},{9,25},{17,1},{25,9},{2,18},{10... | collective-permute-start | bytes 196616 | tf_op jit(solution)/shard_map/ppermute | solution.py:253
  16.2 2.5 %shard_map.69 = (bf16[512,2304]{1,0:T(8,128)(2,1)S(1)}, bf16[512,2304]{1,0:T(8,128)(2,1)S(1)}, bf16[2304,512]{1,0:T(8,128)(2,1)S(1)}, bf16[2304,512]{1,0:T(8,128)(2,1)S(1)}, f32[1,512]{1,0:T(1,128)S(1)}) custom-call(f32[4608,128]{1,0:T(8,128)S(1)} %bitcast.12, f32[4608,128]{1,0:T(8,128)S(1)} %collective-permute-done.8.other), custom_call_target="tpu_custom_call" | custom-call | flops 301989888 | bytes 14157824 | tf_op jit(solution)/shard_map/pallas_call | solution.py:44
  18.7 2.2 %collective-permute-done.5.refs_2_ = f32[32,512]{1,0:T(8,128)S(1)} collective-permute-done((f32[32,512]{1,0:T(8,128)S(1)}, f32[32,512]{1,0:T(8,128)S(1)}, u32[]{:S(2)}, u32[]{:S(2)}) %collective-permute-start.5) | collective-permute-done | bytes 65568 | tf_op jit(solution)/shard_map/ppermute | solution.py:253
  20.9 0.3 collective-permute-done.6.refs_3_
  21.3 0.9 %shard_map.70 = (f32[32,512]{1,0:T(8,128)S(1)}, f32[32,1152]{1,0:T(8,128)S(1)}, f32[32,1152]{1,0:T(8,128)S(1)}) custom-call(f32[32,512]{1,0:T(8,128)S(1)} %shard_map.68.refs_0_, f32[32,512]{1,0:T(8,128)S(1)} %collective-permute-done.4.refs_1_, f32[32,512]{1,0:T(8,128)S(1)} %collective-permute-done.5.refs_2_, f32[32,512]{1,0:T(8,128)S(1)} %collective-permute-done.6.refs_3_, ...), custom_call_target="tpu_custom_call" | custom-call | flops 301989888 | bytes 5343232 | tf_op jit(solution)/shard_map/pallas_call | solution.py:44
  22.2 1.3 %collective-permute-start.11 = (f32[32,1152]{1,0:T(8,128)S(1)}, f32[32,1152]{1,0:T(8,128)S(1)}, u32[]{:S(2)}, u32[]{:S(2)}) collective-permute-start(f32[32,1152]{1,0:T(8,128)S(1)} %get-tuple-element.32), channel_id=1, source_target_pairs={{0,4},{1,5},{2,6},{3,7},{4,0},{5,1},{6,2},{7,3},{8,12},{9,13},{10,... | collective-permute-start | bytes 442376 | tf_op jit(solution)/shard_map/ppermute | solution.py:224
  23.5 1.5 %collective-permute-start.9 = (f32[32,1152]{1,0:T(8,128)S(1)}, f32[32,1152]{1,0:T(8,128)S(1)}, u32[]{:S(2)}, u32[]{:S(2)}) collective-permute-start(f32[32,1152]{1,0:T(8,128)S(1)} %get-tuple-element.31), channel_id=1, source_target_pairs={{0,2},{1,3},{2,0},{3,1},{4,6},{5,7},{6,4},{7,5},{8,10},{9,11},{10,... | collective-permute-start | bytes 442376 | tf_op jit(solution)/shard_map/ppermute | solution.py:224
  25.0 2.3 %collective-permute-done.11 = f32[32,1152]{1,0:T(8,128)S(1)} collective-permute-done((f32[32,1152]{1,0:T(8,128)S(1)}, f32[32,1152]{1,0:T(8,128)S(1)}, u32[]{:S(2)}, u32[]{:S(2)}) %collective-permute-start.11) | collective-permute-done | bytes 147488 | tf_op jit(solution)/shard_map/ppermute | solution.py:224
  27.4 1.3 %collective-permute-start.12 = (f32[32,1152]{1,0:T(8,128)S(1)}, f32[32,1152]{1,0:T(8,128)S(1)}, u32[]{:S(2)}, u32[]{:S(2)}) collective-permute-start(f32[32,1152]{1,0:T(8,128)S(1)} %maximum_add_fusion.1.refs_10_), channel_id=1, source_target_pairs={{0,2},{1,3},{2,0},{3,1},{4,6},{5,7},{6,4},{7,5},{8,10},{9,11},{10,... | collective-permute-start | bytes 442376 | tf_op jit(solution)/shard_map/ppermute | solution.py:224
  28.7 1.0 %collective-permute-done.9 = f32[32,1152]{1,0:T(8,128)S(1)} collective-permute-done((f32[32,1152]{1,0:T(8,128)S(1)}, f32[32,1152]{1,0:T(8,128)S(1)}, u32[]{:S(2)}, u32[]{:S(2)}) %collective-permute-start.9) | collective-permute-done | bytes 147488 | tf_op jit(solution)/shard_map/ppermute | solution.py:224
  29.7 0.6 %collective-permute-start.10 = (f32[32,1152]{1,0:T(8,128)S(1)}, f32[32,1152]{1,0:T(8,128)S(1)}, u32[]{:S(2)}, u32[]{:S(2)}) collective-permute-start(f32[32,1152]{1,0:T(8,128)S(1)} %maximum_add_fusion.refs_8_), channel_id=1, source_target_pairs={{0,4},{1,5},{2,6},{3,7},{4,0},{5,1},{6,2},{7,3},{8,12},{9,13},{10,... | collective-permute-start | bytes 442376 | tf_op jit(solution)/shard_map/ppermute | solution.py:224
  30.4 0.2 shard_map.71.turned
  30.6 2.0 %collective-permute-done.12.refs_11_ = f32[32,1152]{1,0:T(8,128)S(1)} collective-permute-done((f32[32,1152]{1,0:T(8,128)S(1)}, f32[32,1152]{1,0:T(8,128)S(1)}, u32[]{:S(2)}, u32[]{:S(2)}) %collective-permute-start.12) | collective-permute-done | bytes 147488 | tf_op jit(solution)/shard_map/ppermute | solution.py:224
  32.6 2.3 %collective-permute-done.10.refs_9_ = f32[32,1152]{1,0:T(8,128)S(1)} collective-permute-done((f32[32,1152]{1,0:T(8,128)S(1)}, f32[32,1152]{1,0:T(8,128)S(1)}, u32[]{:S(2)}, u32[]{:S(2)}) %collective-permute-start.10) | collective-permute-done | bytes 147488 | tf_op jit(solution)/shard_map/ppermute | solution.py:224
  34.9 0.9 %shard_map.72 = f32[32,512]{1,0:T(8,128)S(1)} custom-call(f32[8,2304]{1,0:T(8,128)S(1)} %bitcast.18, f32[8,2304]{1,0:T(8,128)S(1)} %collective-permute-done.refs_1_, f32[8,2304]{1,0:T(8,128)S(1)} %collective-permute-done.1.refs_2_, f32[8,2304]{1,0:T(8,128)S(1)} %collective-permute-done.2.refs_3_, f32[1,2304]{1,0:T(1,128)S(1)} %copy-done.2, ...), custom_call_target="tpu_custom_call" | custom-call | flops 301989888 | bytes 5680128 | tf_op jit(solution)/shard_map/pallas_call | solution.py:44
  35.8 1.7 %collective-permute-start.13 = (f32[32,512]{1,0:T(8,128)S(1)}, f32[32,512]{1,0:T(8,128)S(1)}, u32[]{:S(2)}, u32[]{:S(2)}) collective-permute-start(f32[32,512]{1,0:T(8,128)S(1)} %shard_map.72), channel_id=1, source_target_pairs={{0,24},{8,16},{16,8},{24,0},{1,25},{9,17},{17,9},{25,1},{2,26},{10... | collective-permute-start | bytes 196616 | tf_op jit(solution)/shard_map/ppermute | solution.py:253
  37.6 0.2 collective-permute-start.14
  37.8 2.4 %collective-permute-start.15 = (f32[32,512]{1,0:T(8,128)S(1)}, f32[32,512]{1,0:T(8,128)S(1)}, u32[]{:S(2)}, u32[]{:S(2)}) collective-permute-start(f32[32,512]{1,0:T(8,128)S(1)} %shard_map.72), channel_id=1, source_target_pairs={{0,16},{8,24},{16,0},{24,8},{1,17},{9,25},{17,1},{25,9},{2,18},{10... | collective-permute-start | bytes 196616 | tf_op jit(solution)/shard_map/ppermute | solution.py:253
  40.3 1.8 %collective-permute-done.13 = f32[32,512]{1,0:T(8,128)S(1)} collective-permute-done((f32[32,512]{1,0:T(8,128)S(1)}, f32[32,512]{1,0:T(8,128)S(1)}, u32[]{:S(2)}, u32[]{:S(2)}) %collective-permute-start.13) | collective-permute-done | bytes 65568 | tf_op jit(solution)/shard_map/ppermute | solution.py:253
  42.0 1.2 %collective-permute-done.14 = f32[32,512]{1,0:T(8,128)S(1)} collective-permute-done((f32[32,512]{1,0:T(8,128)S(1)}, f32[32,512]{1,0:T(8,128)S(1)}, u32[]{:S(2)}, u32[]{:S(2)}) %collective-permute-start.14) | collective-permute-done | bytes 65568 | tf_op jit(solution)/shard_map/ppermute | solution.py:253
  43.3 0.1 collective-permute-start.16
  43.4 1.2 %collective-permute-done.16.theirs = f32[32,256]{1,0:T(8,128)S(1)} collective-permute-done((f32[32,256]{1,0:T(8,128)S(1)}, f32[32,256]{1,0:T(8,128)S(1)}, u32[]{:S(2)}, u32[]{:S(2)}) %collective-permute-start.16) | collective-permute-done | bytes 32800 | tf_op jit(solution)/shard_map/ppermute | solution.py:221
  44.6 2.3 %weight_gradient.1 = (f32[2304,256]{1,0:T(8,128)}, f32[1,256]{1,0:T(1,128)}) custom-call(bf16[2304,256]{1,0:T(8,128)(2,1)S(1)} %shard_map.71.turned, f32[32,256]{1,0:T(8,128)S(1)} %get-tuple-element.53.mine, f32[32,256]{1,0:T(8,128)S(1)} %collective-permute-done.16.theirs), custom_call_target="tpu_custom_call" | custom-call | flops 301989888 | bytes 3538944 | tf_op jit(solution)/shard_map/weight_gradient/pallas_call | solution.py:191
  (31 shorter events, 0.2 us)
Async XLA Ops:
  0.6 7.1 %collective-permute-start = (f32[8,2304]{1,0:T(8,128)}, f32[8,2304]{1,0:T(8,128)S(1)}, u32[]{:S(2)}, u32[]{:S(2)}) collective-permute-start(f32[8,2304]{1,0:T(8,128)} %bitcast.13), channel_id=1, source_target_pairs={{0,2},{1,3},{2,0},{3,1},{4,6},{5,7},{6,4},{7,5},{8,10},{9,11},{10,... | collective-permute-start | bytes 221192 | tf_op jit(solution)/shard_map/ppermute | solution.py:224
  3.7 4.6 %collective-permute-start.1 = (f32[8,2304]{1,0:T(8,128)}, f32[8,2304]{1,0:T(8,128)S(1)}, u32[]{:S(2)}, u32[]{:S(2)}) collective-permute-start(f32[8,2304]{1,0:T(8,128)} %bitcast.14), channel_id=1, source_target_pairs={{0,4},{1,5},{2,6},{3,7},{4,0},{5,1},{6,2},{7,3},{8,12},{9,13},{10,... | collective-permute-start | bytes 221192 | tf_op jit(solution)/shard_map/ppermute | solution.py:224
  5.2 5.5 %collective-permute-start.2 = (f32[8,2304]{1,0:T(8,128)}, f32[8,2304]{1,0:T(8,128)S(1)}, u32[]{:S(2)}, u32[]{:S(2)}) collective-permute-start(f32[8,2304]{1,0:T(8,128)} %bitcast.15), channel_id=1, source_target_pairs={{0,6},{1,7},{2,4},{3,5},{4,2},{5,3},{6,0},{7,1},{8,14},{9,15},{10,... | collective-permute-start | bytes 221192 | tf_op jit(solution)/shard_map/ppermute | solution.py:224
  5.2 5.5 %collective-permute-start.3 = (f32[2304,256]{1,0:T(8,128)}, f32[2304,256]{1,0:T(8,128)S(1)}, u32[]{:S(2)}, u32[]{:S(2)}) collective-permute-start(f32[2304,256]{1,0:T(8,128)} %bitcast.20), channel_id=1, source_target_pairs={{0,1},{1,0},{2,3},{3,2},{4,5},{5,4},{6,7},{7,6},{8,9},{9,8},{10,11... | collective-permute-start | bytes 7077896 | tf_op jit(solution)/shard_map/ppermute | solution.py:221
  5.2 2.5 %copy-start.1 = (f32[1,8,2304]{2,1,0:T(8,128)S(1)}, f32[1,8,2304]{2,1,0:T(8,128)}, u32[]{:S(2)}) copy-start(f32[1,8,2304]{2,1,0:T(8,128)} %param.5) | copy-start | bytes 221188
  5.2 11.0 %collective-permute-start.8 = (f32[4608,128]{1,0:T(8,128)}, f32[4608,128]{1,0:T(8,128)S(1)}, u32[]{:S(2)}, u32[]{:S(2)}) collective-permute-start(f32[4608,128]{1,0:T(8,128)} %bitcast.11), channel_id=1, source_target_pairs={{0,1},{1,0},{2,3},{3,2},{4,5},{5,4},{6,7},{7,6},{8,9},{9,8},{10,11... | collective-permute-start | bytes 7077896 | tf_op jit(solution)/shard_map/ppermute | solution.py:221
  10.7 1.0 %copy-start.3 = (f32[256]{0:T(256)S(1)}, f32[256]{0:T(256)}, u32[]{:S(2)}) copy-start(f32[256]{0:T(256)} %param.7) | copy-start | bytes 3076
  10.7 5.5 %copy-start = (f32[256,1,2304]{2,1,0:T(1,128)S(1)}, f32[256,1,2304]{2,1,0:T(1,128)}, u32[]{:S(2)}) copy-start(f32[256,1,2304]{2,1,0:T(1,128)} %param.8) | copy-start | bytes 7077892
  11.6 9.6 %collective-permute-start.7 = (f32[40,2304]{1,0:T(8,128)S(1)}, f32[40,2304]{1,0:T(8,128)S(1)}, u32[]{:S(2)}, u32[]{:S(2)}) collective-permute-start(f32[40,2304]{1,0:T(8,128)S(1)} %pad_dynamic-update-slice_fusion), channel_id=1, source_target_pairs={{0,1},{1,0},{2,3},{3,2},{4,5},{5,4},{6,7},{7,6},{8,9},{9,8},{10,11... | collective-permute-start | bytes 1105928 | tf_op jit(solution)/shard_map/ppermute | solution.py:221
  11.7 7.0 %collective-permute-start.4 = (f32[32,512]{1,0:T(8,128)S(1)}, f32[32,512]{1,0:T(8,128)S(1)}, u32[]{:S(2)}, u32[]{:S(2)}) collective-permute-start(f32[32,512]{1,0:T(8,128)S(1)} %shard_map.68.refs_0_), channel_id=1, source_target_pairs={{0,24},{8,16},{16,8},{24,0},{1,25},{9,17},{17,9},{25,1},{2,26},{10... | collective-permute-start | bytes 196616 | tf_op jit(solution)/shard_map/ppermute | solution.py:253
  15.4 5.5 %collective-permute-start.5 = (f32[32,512]{1,0:T(8,128)S(1)}, f32[32,512]{1,0:T(8,128)S(1)}, u32[]{:S(2)}, u32[]{:S(2)}) collective-permute-start(f32[32,512]{1,0:T(8,128)S(1)} %shard_map.68.refs_0_), channel_id=1, source_target_pairs={{0,8},{8,0},{16,24},{24,16},{1,9},{9,1},{17,25},{25,17},{2,10},{10... | collective-permute-start | bytes 196616 | tf_op jit(solution)/shard_map/ppermute | solution.py:253
  15.4 5.9 %collective-permute-start.6 = (f32[32,512]{1,0:T(8,128)S(1)}, f32[32,512]{1,0:T(8,128)S(1)}, u32[]{:S(2)}, u32[]{:S(2)}) collective-permute-start(f32[32,512]{1,0:T(8,128)S(1)} %shard_map.68.refs_0_), channel_id=1, source_target_pairs={{0,16},{8,24},{16,0},{24,8},{1,17},{9,25},{17,1},{25,9},{2,18},{10... | collective-permute-start | bytes 196616 | tf_op jit(solution)/shard_map/ppermute | solution.py:253
  22.2 12.8 %copy-start.2 = (f32[1,2304]{1,0:T(1,128)S(1)}, f32[1,2304]{1,0:T(1,128)}, u32[]{:S(2)}) copy-start(f32[1,2304]{1,0:T(1,128)} %refs_4_.1) | copy-start | bytes 27652
  22.2 5.2 %collective-permute-start.11 = (f32[32,1152]{1,0:T(8,128)S(1)}, f32[32,1152]{1,0:T(8,128)S(1)}, u32[]{:S(2)}, u32[]{:S(2)}) collective-permute-start(f32[32,1152]{1,0:T(8,128)S(1)} %get-tuple-element.32), channel_id=1, source_target_pairs={{0,4},{1,5},{2,6},{3,7},{4,0},{5,1},{6,2},{7,3},{8,12},{9,13},{10,... | collective-permute-start | bytes 442376 | tf_op jit(solution)/shard_map/ppermute | solution.py:224
  23.5 6.2 %collective-permute-start.9 = (f32[32,1152]{1,0:T(8,128)S(1)}, f32[32,1152]{1,0:T(8,128)S(1)}, u32[]{:S(2)}, u32[]{:S(2)}) collective-permute-start(f32[32,1152]{1,0:T(8,128)S(1)} %get-tuple-element.31), channel_id=1, source_target_pairs={{0,2},{1,3},{2,0},{3,1},{4,6},{5,7},{6,4},{7,5},{8,10},{9,11},{10,... | collective-permute-start | bytes 442376 | tf_op jit(solution)/shard_map/ppermute | solution.py:224
  27.4 5.2 %collective-permute-start.12 = (f32[32,1152]{1,0:T(8,128)S(1)}, f32[32,1152]{1,0:T(8,128)S(1)}, u32[]{:S(2)}, u32[]{:S(2)}) collective-permute-start(f32[32,1152]{1,0:T(8,128)S(1)} %maximum_add_fusion.1.refs_10_), channel_id=1, source_target_pairs={{0,2},{1,3},{2,0},{3,1},{4,6},{5,7},{6,4},{7,5},{8,10},{9,11},{10,... | collective-permute-start | bytes 442376 | tf_op jit(solution)/shard_map/ppermute | solution.py:224
  29.7 5.2 %collective-permute-start.10 = (f32[32,1152]{1,0:T(8,128)S(1)}, f32[32,1152]{1,0:T(8,128)S(1)}, u32[]{:S(2)}, u32[]{:S(2)}) collective-permute-start(f32[32,1152]{1,0:T(8,128)S(1)} %maximum_add_fusion.refs_8_), channel_id=1, source_target_pairs={{0,4},{1,5},{2,6},{3,7},{4,0},{5,1},{6,2},{7,3},{8,12},{9,13},{10,... | collective-permute-start | bytes 442376 | tf_op jit(solution)/shard_map/ppermute | solution.py:224
  35.8 6.2 %collective-permute-start.13 = (f32[32,512]{1,0:T(8,128)S(1)}, f32[32,512]{1,0:T(8,128)S(1)}, u32[]{:S(2)}, u32[]{:S(2)}) collective-permute-start(f32[32,512]{1,0:T(8,128)S(1)} %shard_map.72), channel_id=1, source_target_pairs={{0,24},{8,16},{16,8},{24,0},{1,25},{9,17},{17,9},{25,1},{2,26},{10... | collective-permute-start | bytes 196616 | tf_op jit(solution)/shard_map/ppermute | solution.py:253
  37.6 5.7 %collective-permute-start.14 = (f32[32,512]{1,0:T(8,128)S(1)}, f32[32,512]{1,0:T(8,128)S(1)}, u32[]{:S(2)}, u32[]{:S(2)}) collective-permute-start(f32[32,512]{1,0:T(8,128)S(1)} %shard_map.72), channel_id=1, source_target_pairs={{0,8},{8,0},{16,24},{24,16},{1,9},{9,1},{17,25},{25,17},{2,10},{10... | collective-permute-start | bytes 196616 | tf_op jit(solution)/shard_map/ppermute | solution.py:253
  37.8 5.4 %collective-permute-start.15 = (f32[32,512]{1,0:T(8,128)S(1)}, f32[32,512]{1,0:T(8,128)S(1)}, u32[]{:S(2)}, u32[]{:S(2)}) collective-permute-start(f32[32,512]{1,0:T(8,128)S(1)} %shard_map.72), channel_id=1, source_target_pairs={{0,16},{8,24},{16,0},{24,8},{1,17},{9,25},{17,1},{25,9},{2,18},{10... | collective-permute-start | bytes 196616 | tf_op jit(solution)/shard_map/ppermute | solution.py:253
  43.3 1.3 %collective-permute-start.16 = (f32[32,256]{1,0:T(8,128)S(1)}, f32[32,256]{1,0:T(8,128)S(1)}, u32[]{:S(2)}, u32[]{:S(2)}) collective-permute-start(f32[32,256]{1,0:T(8,128)S(1)} %get-tuple-element.52), channel_id=1, source_target_pairs={{0,1},{1,0},{2,3},{3,2},{4,5},{5,4},{6,7},{7,6},{8,9},{9,8},{10,11... | collective-permute-start | bytes 98312 | tf_op jit(solution)/shard_map/ppermute | solution.py:221

commit v2 on v1

--- a/solution.py
+++ b/solution.py
@@ -61,8 +61,8 @@
     left = stacked(rows_of(blocks))
     width = other.shape[1]
     totals = [None, None]
-    for start in range(0, other.shape[0], CHUNK):
-        here = slice(start, start + CHUNK)
+    for start in range(0, other.shape[0], 768):
+        here = slice(start, start + 768)
         part = left[:, here]
         rights = ((own_high[here, :], own_low[here, :]), split(other[here, :]))
         for at in range(2):
@@ -186,7 +186,7 @@
 def weight_gradient(turned, mine, theirs):
     features, depth = turned.shape
     width = mine.shape[1]
-    steps = next(n for n in (6, 4, 3, 2, 1) if features % (8 * n) == 0)
+    steps = next(n for n in (3, 2, 1) if features % (8 * n) == 0)
     vmem = pl.BlockSpec(memory_space=pltpu.VMEM)
     return pl.pallas_call(
         functools.partial(weight_kernel, features // steps),
@@ -301,7 +301,6 @@
         work,
     )
     masks, pieces = sum_chips(shares, rows)
-    pieces, turned = lax.optimization_barrier((pieces, turned))
     (grad_part,) = call(
         functools.partial(gradient_kernel, len(gathered), masks, rows),
         [((tokens, 2 * width), F32)],

time: 47 us -> 47 us (level)
  no operation moved by 1% of the time
where the time goes in v2:
time: 47 us; the launch traced here: 46.8 us
  starting transfers between devices  18.9 us (40%)
  waiting for transfers between devices  17.3 us (37%)
  Pallas kernels  7.69 us (16%)
  other arithmetic  2.1 us (4%)
  between operations  0.8 us (2%)
    ppermute x7, waiting for transfers between devices, to_chip(): return lax.ppermute(x, 'latent', [(i, i ^ 2 * k) for i in range(latents)])  10.7 us
    ppermute x7, starting transfers between devices, to_chip(): return lax.ppermute(x, 'latent', [(i, i ^ 2 * k) for i in range(latents)])  9.35 us
    ppermute x6, starting transfers between devices, from_layers(): got.append(lax.ppermute(x, 'layer', pairs))  8.86 us
    ppermute x6, waiting for transfers between devices, from_layers(): got.append(lax.ppermute(x, 'layer', pairs))  5.57 us
    pallas_call x5, Pallas kernels, call_in_vmem(): pl.pallas_call(kernel, out_shape=outs, in_specs=[pl.BlockSpec(memory_spac...  5.44 us
    pallas_call x1, Pallas kernels, weight_gradient(): pl.pallas_call(functools.partial(weight_kernel, features // steps), out_s...  2.25 us
    convert_element_type x1, other arithmetic, on_device(): own_high, own_low = (rounded.astype(BF16), (enc - rounded).astype(BF16))  2.02 us
    ppermute x4, waiting for transfers between devices, to_partner(): return lax.ppermute(x, 'latent', [(i, i ^ 1) for i in range(latents)])  0.96 us
  transfers between devices with their start and end apart: 17, of which 11 were waited for; matrix products, arithmetic and copies ran while one was open for 5% of the time, Pallas kernels for 8%

profile of v2, /device:TPU:0, one launch (start us, length us, event | category | flops | bytes accessed | tf_op | source)
XLA Modules:
  0.0 46.8 jit_solution(17672521377753414203)
XLA Ops:
  0.6 3.0 %collective-permute-start = (f32[8,2304]{1,0:T(8,128)}, f32[8,2304]{1,0:T(8,128)S(1)}, u32[]{:S(2)}, u32[]{:S(2)}) collective-permute-start(f32[8,2304]{1,0:T(8,128)} %bitcast.13), channel_id=1, source_target_pairs={{0,2},{1,3},{2,0},{3,1},{4,6},{5,7},{6,4},{7,5},{8,10},{9,11},{10,... | collective-permute-start | bytes 221192 | tf_op jit(solution)/shard_map/ppermute | solution.py:224
  3.7 1.5 %collective-permute-start.1 = (f32[8,2304]{1,0:T(8,128)}, f32[8,2304]{1,0:T(8,128)S(1)}, u32[]{:S(2)}, u32[]{:S(2)}) collective-permute-start(f32[8,2304]{1,0:T(8,128)} %bitcast.14), channel_id=1, source_target_pairs={{0,4},{1,5},{2,6},{3,7},{4,0},{5,1},{6,2},{7,3},{8,12},{9,13},{10,... | collective-permute-start | bytes 221192 | tf_op jit(solution)/shard_map/ppermute | solution.py:224
  5.2 0.5 %collective-permute-start.8 = (f32[4608,128]{1,0:T(8,128)}, f32[4608,128]{1,0:T(8,128)S(1)}, u32[]{:S(2)}, u32[]{:S(2)}) collective-permute-start(f32[4608,128]{1,0:T(8,128)} %bitcast.11), channel_id=1, source_target_pairs={{0,1},{1,0},{2,3},{3,2},{4,5},{5,4},{6,7},{7,6},{8,9},{9,8},{10,11... | collective-permute-start | bytes 7077896 | tf_op jit(solution)/shard_map/ppermute | solution.py:221
  5.7 2.0 %fusion = (bf16[2304,256]{1,0:T(8,128)(2,1)S(1)}, bf16[2304,256]{1,0:T(8,128)(2,1)S(1)}) fusion(f32[1,2304,256]{2,1,0:T(8,128)} %param.6), kind=kLoop, calls=%fused_computation.2 | loop fusion | flops 2359296 | bytes 4718592 | tf_op jit(solution)/shard_map/convert_element_type | solution.py:267
  7.8 0.4 collective-permute-done.1.refs_2_
  8.2 2.4 %collective-permute-done.2.refs_3_ = f32[8,2304]{1,0:T(8,128)S(1)} collective-permute-done((f32[8,2304]{1,0:T(8,128)}, f32[8,2304]{1,0:T(8,128)S(1)}, u32[]{:S(2)}, u32[]{:S(2)}) %collective-permute-start.2) | collective-permute-done | bytes 73760 | tf_op jit(solution)/shard_map/ppermute | solution.py:224
  10.7 0.9 %shard_map.68.refs_0_ = f32[32,512]{1,0:T(8,128)S(1)} custom-call(f32[8,2304]{1,0:T(8,128)S(1)} %bitcast.16, f32[8,2304]{1,0:T(8,128)S(1)} %collective-permute-done.refs_1_, f32[8,2304]{1,0:T(8,128)S(1)} %collective-permute-done.1.refs_2_, f32[8,2304]{1,0:T(8,128)S(1)} %collective-permute-done.2.refs_3_, bf16[2304,256]{1,0:T(8,128)(2,1)S(1)} %get-tuple-element.35.refs_4_, ...), custom_call_target="tpu_custom_call" | custom-call | flops 301989888 | bytes 5079040 | tf_op jit(solution)/shard_map/pallas_call | solution.py:44
  11.6 0.1 collective-permute-start.7
  11.7 3.7 %collective-permute-start.4 = (f32[32,512]{1,0:T(8,128)S(1)}, f32[32,512]{1,0:T(8,128)S(1)}, u32[]{:S(2)}, u32[]{:S(2)}) collective-permute-start(f32[32,512]{1,0:T(8,128)S(1)} %shard_map.68.refs_0_), channel_id=1, source_target_pairs={{0,24},{8,16},{16,8},{24,0},{1,25},{9,17},{17,9},{25,1},{2,26},{10... | collective-permute-start | bytes 196616 | tf_op jit(solution)/shard_map/ppermute | solution.py:253
  15.4 0.8 %collective-permute-start.6 = (f32[32,512]{1,0:T(8,128)S(1)}, f32[32,512]{1,0:T(8,128)S(1)}, u32[]{:S(2)}, u32[]{:S(2)}) collective-permute-start(f32[32,512]{1,0:T(8,128)S(1)} %shard_map.68.refs_0_), channel_id=1, source_target_pairs={{0,16},{8,24},{16,0},{24,8},{1,17},{9,25},{17,1},{25,9},{2,18},{10... | collective-permute-start | bytes 196616 | tf_op jit(solution)/shard_map/ppermute | solution.py:253
  16.2 2.5 %shard_map.70 = (bf16[512,2304]{1,0:T(8,128)(2,1)S(1)}, bf16[512,2304]{1,0:T(8,128)(2,1)S(1)}, bf16[2304,512]{1,0:T(8,128)(2,1)S(1)}, bf16[2304,512]{1,0:T(8,128)(2,1)S(1)}, f32[1,512]{1,0:T(1,128)S(1)}) custom-call(f32[4608,128]{1,0:T(8,128)S(1)} %bitcast.12, f32[4608,128]{1,0:T(8,128)S(1)} %collective-permute-done.8.other), custom_call_target="tpu_custom_call" | custom-call | flops 301989888 | bytes 14157824 | tf_op jit(solution)/shard_map/pallas_call | solution.py:44
  18.7 2.2 %collective-permute-done.5.refs_2_ = f32[32,512]{1,0:T(8,128)S(1)} collective-permute-done((f32[32,512]{1,0:T(8,128)S(1)}, f32[32,512]{1,0:T(8,128)S(1)}, u32[]{:S(2)}, u32[]{:S(2)}) %collective-permute-start.5) | collective-permute-done | bytes 65568 | tf_op jit(solution)/shard_map/ppermute | solution.py:253
  20.9 0.3 collective-permute-done.6.refs_3_
  21.3 0.9 %shard_map.71 = (f32[32,512]{1,0:T(8,128)S(1)}, f32[32,1152]{1,0:T(8,128)S(1)}, f32[32,1152]{1,0:T(8,128)S(1)}) custom-call(f32[32,512]{1,0:T(8,128)S(1)} %shard_map.68.refs_0_, f32[32,512]{1,0:T(8,128)S(1)} %collective-permute-done.4.refs_1_, f32[32,512]{1,0:T(8,128)S(1)} %collective-permute-done.5.refs_2_, f32[32,512]{1,0:T(8,128)S(1)} %collective-permute-done.6.refs_3_, ...), custom_call_target="tpu_custom_call" | custom-call | flops 301989888 | bytes 5343232 | tf_op jit(solution)/shard_map/pallas_call | solution.py:44
  22.2 1.3 %collective-permute-start.11 = (f32[32,1152]{1,0:T(8,128)S(1)}, f32[32,1152]{1,0:T(8,128)S(1)}, u32[]{:S(2)}, u32[]{:S(2)}) collective-permute-start(f32[32,1152]{1,0:T(8,128)S(1)} %get-tuple-element.30), channel_id=1, source_target_pairs={{0,4},{1,5},{2,6},{3,7},{4,0},{5,1},{6,2},{7,3},{8,12},{9,13},{10,... | collective-permute-start | bytes 442376 | tf_op jit(solution)/shard_map/ppermute | solution.py:224
  23.5 1.5 %collective-permute-start.9 = (f32[32,1152]{1,0:T(8,128)S(1)}, f32[32,1152]{1,0:T(8,128)S(1)}, u32[]{:S(2)}, u32[]{:S(2)}) collective-permute-start(f32[32,1152]{1,0:T(8,128)S(1)} %get-tuple-element.29), channel_id=1, source_target_pairs={{0,2},{1,3},{2,0},{3,1},{4,6},{5,7},{6,4},{7,5},{8,10},{9,11},{10,... | collective-permute-start | bytes 442376 | tf_op jit(solution)/shard_map/ppermute | solution.py:224
  25.0 2.4 %collective-permute-done.11 = f32[32,1152]{1,0:T(8,128)S(1)} collective-permute-done((f32[32,1152]{1,0:T(8,128)S(1)}, f32[32,1152]{1,0:T(8,128)S(1)}, u32[]{:S(2)}, u32[]{:S(2)}) %collective-permute-start.11) | collective-permute-done | bytes 147488 | tf_op jit(solution)/shard_map/ppermute | solution.py:224
  27.4 1.3 %collective-permute-start.12 = (f32[32,1152]{1,0:T(8,128)S(1)}, f32[32,1152]{1,0:T(8,128)S(1)}, u32[]{:S(2)}, u32[]{:S(2)}) collective-permute-start(f32[32,1152]{1,0:T(8,128)S(1)} %maximum_add_fusion.1.refs_10_), channel_id=1, source_target_pairs={{0,2},{1,3},{2,0},{3,1},{4,6},{5,7},{6,4},{7,5},{8,10},{9,11},{10,... | collective-permute-start | bytes 442376 | tf_op jit(solution)/shard_map/ppermute | solution.py:224
  28.7 1.0 %collective-permute-done.9 = f32[32,1152]{1,0:T(8,128)S(1)} collective-permute-done((f32[32,1152]{1,0:T(8,128)S(1)}, f32[32,1152]{1,0:T(8,128)S(1)}, u32[]{:S(2)}, u32[]{:S(2)}) %collective-permute-start.9) | collective-permute-done | bytes 147488 | tf_op jit(solution)/shard_map/ppermute | solution.py:224
  29.7 0.6 %collective-permute-start.10 = (f32[32,1152]{1,0:T(8,128)S(1)}, f32[32,1152]{1,0:T(8,128)S(1)}, u32[]{:S(2)}, u32[]{:S(2)}) collective-permute-start(f32[32,1152]{1,0:T(8,128)S(1)} %maximum_add_fusion.refs_8_), channel_id=1, source_target_pairs={{0,4},{1,5},{2,6},{3,7},{4,0},{5,1},{6,2},{7,3},{8,12},{9,13},{10,... | collective-permute-start | bytes 442376 | tf_op jit(solution)/shard_map/ppermute | solution.py:224
  30.4 2.2 %collective-permute-done.12.refs_11_ = f32[32,1152]{1,0:T(8,128)S(1)} collective-permute-done((f32[32,1152]{1,0:T(8,128)S(1)}, f32[32,1152]{1,0:T(8,128)S(1)}, u32[]{:S(2)}, u32[]{:S(2)}) %collective-permute-start.12) | collective-permute-done | bytes 147488 | tf_op jit(solution)/shard_map/ppermute | solution.py:224
  32.6 2.3 %collective-permute-done.10.refs_9_ = f32[32,1152]{1,0:T(8,128)S(1)} collective-permute-done((f32[32,1152]{1,0:T(8,128)S(1)}, f32[32,1152]{1,0:T(8,128)S(1)}, u32[]{:S(2)}, u32[]{:S(2)}) %collective-permute-start.10) | collective-permute-done | bytes 147488 | tf_op jit(solution)/shard_map/ppermute | solution.py:224
  35.0 0.9 %shard_map.72 = f32[32,512]{1,0:T(8,128)S(1)} custom-call(f32[8,2304]{1,0:T(8,128)S(1)} %bitcast.17, f32[8,2304]{1,0:T(8,128)S(1)} %collective-permute-done.refs_1_, f32[8,2304]{1,0:T(8,128)S(1)} %collective-permute-done.1.refs_2_, f32[8,2304]{1,0:T(8,128)S(1)} %collective-permute-done.2.refs_3_, f32[1,2304]{1,0:T(1,128)S(1)} %copy-done.2, ...), custom_call_target="tpu_custom_call" | custom-call | flops 301989888 | bytes 5680128 | tf_op jit(solution)/shard_map/pallas_call | solution.py:44
  35.9 1.7 %collective-permute-start.13 = (f32[32,512]{1,0:T(8,128)S(1)}, f32[32,512]{1,0:T(8,128)S(1)}, u32[]{:S(2)}, u32[]{:S(2)}) collective-permute-start(f32[32,512]{1,0:T(8,128)S(1)} %shard_map.72), channel_id=1, source_target_pairs={{0,24},{8,16},{16,8},{24,0},{1,25},{9,17},{17,9},{25,1},{2,26},{10... | collective-permute-start | bytes 196616 | tf_op jit(solution)/shard_map/ppermute | solution.py:253
  37.6 0.2 collective-permute-start.14
  37.8 2.4 %collective-permute-start.15 = (f32[32,512]{1,0:T(8,128)S(1)}, f32[32,512]{1,0:T(8,128)S(1)}, u32[]{:S(2)}, u32[]{:S(2)}) collective-permute-start(f32[32,512]{1,0:T(8,128)S(1)} %shard_map.72), channel_id=1, source_target_pairs={{0,16},{8,24},{16,0},{24,8},{1,17},{9,25},{17,1},{25,9},{2,18},{10... | collective-permute-start | bytes 196616 | tf_op jit(solution)/shard_map/ppermute | solution.py:253
  40.3 1.8 %collective-permute-done.13 = f32[32,512]{1,0:T(8,128)S(1)} collective-permute-done((f32[32,512]{1,0:T(8,128)S(1)}, f32[32,512]{1,0:T(8,128)S(1)}, u32[]{:S(2)}, u32[]{:S(2)}) %collective-permute-start.13) | collective-permute-done | bytes 65568 | tf_op jit(solution)/shard_map/ppermute | solution.py:253
  42.1 1.2 %collective-permute-done.14 = f32[32,512]{1,0:T(8,128)S(1)} collective-permute-done((f32[32,512]{1,0:T(8,128)S(1)}, f32[32,512]{1,0:T(8,128)S(1)}, u32[]{:S(2)}, u32[]{:S(2)}) %collective-permute-start.14) | collective-permute-done | bytes 65568 | tf_op jit(solution)/shard_map/ppermute | solution.py:253
  43.3 0.1 collective-permute-start.16
  43.4 0.2 shard_map.69.turned
  43.6 1.0 %collective-permute-done.16.theirs = f32[32,256]{1,0:T(8,128)S(1)} collective-permute-done((f32[32,256]{1,0:T(8,128)S(1)}, f32[32,256]{1,0:T(8,128)S(1)}, u32[]{:S(2)}, u32[]{:S(2)}) %collective-permute-start.16) | collective-permute-done | bytes 32800 | tf_op jit(solution)/shard_map/ppermute | solution.py:221
  44.6 2.3 %weight_gradient.1 = (f32[2304,256]{1,0:T(8,128)}, f32[1,256]{1,0:T(1,128)}) custom-call(bf16[2304,256]{1,0:T(8,128)(2,1)S(1)} %shard_map.69.turned, f32[32,256]{1,0:T(8,128)S(1)} %get-tuple-element.43.mine, f32[32,256]{1,0:T(8,128)S(1)} %collective-permute-done.16.theirs), custom_call_target="tpu_custom_call" | custom-call | flops 301989888 | bytes 3538944 | tf_op jit(solution)/shard_map/weight_gradient/pallas_call | solution.py:191
  (31 shorter events, 0.2 us)
Async XLA Ops:
  0.6 7.1 %collective-permute-start = (f32[8,2304]{1,0:T(8,128)}, f32[8,2304]{1,0:T(8,128)S(1)}, u32[]{:S(2)}, u32[]{:S(2)}) collective-permute-start(f32[8,2304]{1,0:T(8,128)} %bitcast.13), channel_id=1, source_target_pairs={{0,2},{1,3},{2,0},{3,1},{4,6},{5,7},{6,4},{7,5},{8,10},{9,11},{10,... | collective-permute-start | bytes 221192 | tf_op jit(solution)/shard_map/ppermute | solution.py:224
  3.7 4.6 %collective-permute-start.1 = (f32[8,2304]{1,0:T(8,128)}, f32[8,2304]{1,0:T(8,128)S(1)}, u32[]{:S(2)}, u32[]{:S(2)}) collective-permute-start(f32[8,2304]{1,0:T(8,128)} %bitcast.14), channel_id=1, source_target_pairs={{0,4},{1,5},{2,6},{3,7},{4,0},{5,1},{6,2},{7,3},{8,12},{9,13},{10,... | collective-permute-start | bytes 221192 | tf_op jit(solution)/shard_map/ppermute | solution.py:224
  5.2 5.5 %collective-permute-start.2 = (f32[8,2304]{1,0:T(8,128)}, f32[8,2304]{1,0:T(8,128)S(1)}, u32[]{:S(2)}, u32[]{:S(2)}) collective-permute-start(f32[8,2304]{1,0:T(8,128)} %bitcast.15), channel_id=1, source_target_pairs={{0,6},{1,7},{2,4},{3,5},{4,2},{5,3},{6,0},{7,1},{8,14},{9,15},{10,... | collective-permute-start | bytes 221192 | tf_op jit(solution)/shard_map/ppermute | solution.py:224
  5.2 5.5 %collective-permute-start.3 = (f32[2304,256]{1,0:T(8,128)}, f32[2304,256]{1,0:T(8,128)S(1)}, u32[]{:S(2)}, u32[]{:S(2)}) collective-permute-start(f32[2304,256]{1,0:T(8,128)} %bitcast.20), channel_id=1, source_target_pairs={{0,1},{1,0},{2,3},{3,2},{4,5},{5,4},{6,7},{7,6},{8,9},{9,8},{10,11... | collective-permute-start | bytes 7077896 | tf_op jit(solution)/shard_map/ppermute | solution.py:221
  5.2 2.5 %copy-start.1 = (f32[1,8,2304]{2,1,0:T(8,128)S(1)}, f32[1,8,2304]{2,1,0:T(8,128)}, u32[]{:S(2)}) copy-start(f32[1,8,2304]{2,1,0:T(8,128)} %param.5) | copy-start | bytes 221188
  5.2 11.0 %collective-permute-start.8 = (f32[4608,128]{1,0:T(8,128)}, f32[4608,128]{1,0:T(8,128)S(1)}, u32[]{:S(2)}, u32[]{:S(2)}) collective-permute-start(f32[4608,128]{1,0:T(8,128)} %bitcast.11), channel_id=1, source_target_pairs={{0,1},{1,0},{2,3},{3,2},{4,5},{5,4},{6,7},{7,6},{8,9},{9,8},{10,11... | collective-permute-start | bytes 7077896 | tf_op jit(solution)/shard_map/ppermute | solution.py:221
  10.7 1.0 %copy-start.3 = (f32[256]{0:T(256)S(1)}, f32[256]{0:T(256)}, u32[]{:S(2)}) copy-start(f32[256]{0:T(256)} %param.7) | copy-start | bytes 3076
  10.7 5.5 %copy-start = (f32[256,1,2304]{2,1,0:T(1,128)S(1)}, f32[256,1,2304]{2,1,0:T(1,128)}, u32[]{:S(2)}) copy-start(f32[256,1,2304]{2,1,0:T(1,128)} %param.8) | copy-start | bytes 7077892
  11.6 9.6 %collective-permute-start.7 = (f32[40,2304]{1,0:T(8,128)S(1)}, f32[40,2304]{1,0:T(8,128)S(1)}, u32[]{:S(2)}, u32[]{:S(2)}) collective-permute-start(f32[40,2304]{1,0:T(8,128)S(1)} %pad_dynamic-update-slice_fusion), channel_id=1, source_target_pairs={{0,1},{1,0},{2,3},{3,2},{4,5},{5,4},{6,7},{7,6},{8,9},{9,8},{10,11... | collective-permute-start | bytes 1105928 | tf_op jit(solution)/shard_map/ppermute | solution.py:221
  11.7 7.0 %collective-permute-start.4 = (f32[32,512]{1,0:T(8,128)S(1)}, f32[32,512]{1,0:T(8,128)S(1)}, u32[]{:S(2)}, u32[]{:S(2)}) collective-permute-start(f32[32,512]{1,0:T(8,128)S(1)} %shard_map.68.refs_0_), channel_id=1, source_target_pairs={{0,24},{8,16},{16,8},{24,0},{1,25},{9,17},{17,9},{25,1},{2,26},{10... | collective-permute-start | bytes 196616 | tf_op jit(solution)/shard_map/ppermute | solution.py:253
  15.4 5.5 %collective-permute-start.5 = (f32[32,512]{1,0:T(8,128)S(1)}, f32[32,512]{1,0:T(8,128)S(1)}, u32[]{:S(2)}, u32[]{:S(2)}) collective-permute-start(f32[32,512]{1,0:T(8,128)S(1)} %shard_map.68.refs_0_), channel_id=1, source_target_pairs={{0,8},{8,0},{16,24},{24,16},{1,9},{9,1},{17,25},{25,17},{2,10},{10... | collective-permute-start | bytes 196616 | tf_op jit(solution)/shard_map/ppermute | solution.py:253
  15.4 5.9 %collective-permute-start.6 = (f32[32,512]{1,0:T(8,128)S(1)}, f32[32,512]{1,0:T(8,128)S(1)}, u32[]{:S(2)}, u32[]{:S(2)}) collective-permute-start(f32[32,512]{1,0:T(8,128)S(1)} %shard_map.68.refs_0_), channel_id=1, source_target_pairs={{0,16},{8,24},{16,0},{24,8},{1,17},{9,25},{17,1},{25,9},{2,18},{10... | collective-permute-start | bytes 196616 | tf_op jit(solution)/shard_map/ppermute | solution.py:253
  21.3 13.7 %copy-start.2 = (f32[1,2304]{1,0:T(1,128)S(1)}, f32[1,2304]{1,0:T(1,128)}, u32[]{:S(2)}) copy-start(f32[1,2304]{1,0:T(1,128)} %refs_4_.1) | copy-start | bytes 27652
  22.2 5.2 %collective-permute-start.11 = (f32[32,1152]{1,0:T(8,128)S(1)}, f32[32,1152]{1,0:T(8,128)S(1)}, u32[]{:S(2)}, u32[]{:S(2)}) collective-permute-start(f32[32,1152]{1,0:T(8,128)S(1)} %get-tuple-element.30), channel_id=1, source_target_pairs={{0,4},{1,5},{2,6},{3,7},{4,0},{5,1},{6,2},{7,3},{8,12},{9,13},{10,... | collective-permute-start | bytes 442376 | tf_op jit(solution)/shard_map/ppermute | solution.py:224
  23.5 6.2 %collective-permute-start.9 = (f32[32,1152]{1,0:T(8,128)S(1)}, f32[32,1152]{1,0:T(8,128)S(1)}, u32[]{:S(2)}, u32[]{:S(2)}) collective-permute-start(f32[32,1152]{1,0:T(8,128)S(1)} %get-tuple-element.29), channel_id=1, source_target_pairs={{0,2},{1,3},{2,0},{3,1},{4,6},{5,7},{6,4},{7,5},{8,10},{9,11},{10,... | collective-permute-start | bytes 442376 | tf_op jit(solution)/shard_map/ppermute | solution.py:224
  27.4 5.2 %collective-permute-start.12 = (f32[32,1152]{1,0:T(8,128)S(1)}, f32[32,1152]{1,0:T(8,128)S(1)}, u32[]{:S(2)}, u32[]{:S(2)}) collective-permute-start(f32[32,1152]{1,0:T(8,128)S(1)} %maximum_add_fusion.1.refs_10_), channel_id=1, source_target_pairs={{0,2},{1,3},{2,0},{3,1},{4,6},{5,7},{6,4},{7,5},{8,10},{9,11},{10,... | collective-permute-start | bytes 442376 | tf_op jit(solution)/shard_map/ppermute | solution.py:224
  29.7 5.2 %collective-permute-start.10 = (f32[32,1152]{1,0:T(8,128)S(1)}, f32[32,1152]{1,0:T(8,128)S(1)}, u32[]{:S(2)}, u32[]{:S(2)}) collective-permute-start(f32[32,1152]{1,0:T(8,128)S(1)} %maximum_add_fusion.refs_8_), channel_id=1, source_target_pairs={{0,4},{1,5},{2,6},{3,7},{4,0},{5,1},{6,2},{7,3},{8,12},{9,13},{10,... | collective-permute-start | bytes 442376 | tf_op jit(solution)/shard_map/ppermute | solution.py:224
  35.9 6.2 %collective-permute-start.13 = (f32[32,512]{1,0:T(8,128)S(1)}, f32[32,512]{1,0:T(8,128)S(1)}, u32[]{:S(2)}, u32[]{:S(2)}) collective-permute-start(f32[32,512]{1,0:T(8,128)S(1)} %shard_map.72), channel_id=1, source_target_pairs={{0,24},{8,16},{16,8},{24,0},{1,25},{9,17},{17,9},{25,1},{2,26},{10... | collective-permute-start | bytes 196616 | tf_op jit(solution)/shard_map/ppermute | solution.py:253
  37.6 5.7 %collective-permute-start.14 = (f32[32,512]{1,0:T(8,128)S(1)}, f32[32,512]{1,0:T(8,128)S(1)}, u32[]{:S(2)}, u32[]{:S(2)}) collective-permute-start(f32[32,512]{1,0:T(8,128)S(1)} %shard_map.72), channel_id=1, source_target_pairs={{0,8},{8,0},{16,24},{24,16},{1,9},{9,1},{17,25},{25,17},{2,10},{10... | collective-permute-start | bytes 196616 | tf_op jit(solution)/shard_map/ppermute | solution.py:253
  37.8 5.4 %collective-permute-start.15 = (f32[32,512]{1,0:T(8,128)S(1)}, f32[32,512]{1,0:T(8,128)S(1)}, u32[]{:S(2)}, u32[]{:S(2)}) collective-permute-start(f32[32,512]{1,0:T(8,128)S(1)} %shard_map.72), channel_id=1, source_target_pairs={{0,16},{8,24},{16,0},{24,8},{1,17},{9,25},{17,1},{25,9},{2,18},{10... | collective-permute-start | bytes 196616 | tf_op jit(solution)/shard_map/ppermute | solution.py:253
  43.3 1.3 %collective-permute-start.16 = (f32[32,256]{1,0:T(8,128)S(1)}, f32[32,256]{1,0:T(8,128)S(1)}, u32[]{:S(2)}, u32[]{:S(2)}) collective-permute-start(f32[32,256]{1,0:T(8,128)S(1)} %get-tuple-element.42), channel_id=1, source_target_pairs={{0,1},{1,0},{2,3},{3,2},{4,5},{5,4},{6,7},{7,6},{8,9},{9,8},{10,11... | collective-permute-start | bytes 98312 | tf_op jit(solution)/shard_map/ppermute | solution.py:221
